TPU v7x, 16 devices: a whole 2x2x2 slice. The times are simulated.
16 devices in a mesh: tp: 2 (over z), cp: 2 (over y), dp: 4 (over x, core).
Axes of the slice: x: 2, y: 2, z: 2, core: 2. Of those that a mesh axis runs over, the one named last changes fastest.
Arguments:
- hidden: bfloat16 [64, 64, 2048], P('dp', 'cp')
- tokens: int32 [64, 64], P('dp', 'cp')
- seq_lens: int32 [64], P('dp')
- norm_gain: float32 [2048], replicated
- w_head: bfloat16 [2048, 49152], P(None, 'tp')
Outputs:
- output 1: float32 [64, 64], P('dp', 'cp')
- output 2: float32 [], replicated
- output 3: bfloat16 [64, 64, 2048], P('dp', 'cp')
- output 4: float32 [2048], replicated
- output 5: float32 [2048, 49152], P(None, 'tp')
All inputs are finite; a program needn't handle non-finite values.
Results may differ from a plain program's by a relative error of at most 0.001.
Values sent between devices are 32-bit elements.
A program may use at most 1.25 GiB of HBM per device.

v0:
```python
import jax
import jax.numpy as jnp
from jax import lax
from jax.sharding import PartitionSpec as P

NORM_EPS = 1e-5


def solution(mesh):
    cp_size = mesh.shape['cp']
    from_next_pairs = [(cp_idx + 1, cp_idx) for cp_idx in range(cp_size - 1)]
    from_prev_pairs = [(cp_idx - 1, cp_idx) for cp_idx in range(1, cp_size)]

    def local_fn(hidden, tokens, seq_lens, norm_gain, w_head):
        local_len = tokens.shape[1]
        seg_len = local_len // 2
        vocab_local = w_head.shape[1]
        cp_rank = lax.axis_index('cp')
        tp_rank = lax.axis_index('tp')

        next_first = lax.ppermute(tokens[:, 0], 'cp', from_next_pairs)
        prev_second = lax.ppermute(tokens[:, seg_len], 'cp', from_prev_pairs)
        first_end = jnp.where(cp_rank == cp_size - 1, tokens[:, seg_len], next_first)
        labels = jnp.concatenate([tokens[:, 1:seg_len], first_end[:, None], tokens[:, seg_len + 1:], prev_second[:, None]], axis=1)

        seg_pos = jnp.arange(seg_len)
        positions = jnp.concatenate([cp_rank * seg_len + seg_pos, (2 * cp_size - 1 - cp_rank) * seg_len + seg_pos])
        valid_mask = (positions[None, :] + 1 < seq_lens[:, None]).astype(jnp.float32)
        valid_count = lax.psum(jnp.sum(seq_lens - 1).astype(jnp.float32), 'dp')

        h_f32 = hidden.astype(jnp.float32)
        inv_rms = lax.rsqrt(jnp.mean(h_f32 * h_f32, axis=-1, keepdims=True) + NORM_EPS)
        x_hat = h_f32 * inv_rms
        x_norm = (x_hat * norm_gain).astype(jnp.bfloat16)
        logits = jnp.einsum('bsd,dv->bsv', x_norm, w_head, preferred_element_type=jnp.float32)

        glob_max = lax.pmax(jnp.max(logits, axis=-1), 'tp')
        sum_exp = lax.psum(jnp.sum(jnp.exp(logits - glob_max[..., None]), axis=-1), 'tp')
        log_norm = glob_max + jnp.log(sum_exp)
        local_lab = labels - tp_rank * vocab_local
        label_hit = jnp.arange(vocab_local)[None, None, :] == local_lab[..., None]
        target_logit = lax.psum(jnp.sum(jnp.where(label_hit, logits, 0.0), axis=-1), 'tp')
        tok_loss = (log_norm - target_logit) * valid_mask
        loss_mean = lax.psum(jnp.sum(tok_loss), ('cp', 'dp')) / valid_count

        tok_scale = valid_mask / valid_count
        soft_prob = jnp.exp(logits - log_norm[..., None])
        d_logits = ((soft_prob - label_hit.astype(jnp.float32)) * tok_scale[..., None]).astype(jnp.bfloat16)
        dx_norm = lax.psum(jnp.einsum('bsv,dv->bsd', d_logits, w_head, preferred_element_type=jnp.float32), 'tp')
        d_head = lax.psum(jnp.einsum('bsd,bsv->dv', x_norm, d_logits, preferred_element_type=jnp.float32), ('cp', 'dp'))
        d_gain = lax.psum(jnp.sum(dx_norm * x_hat, axis=(0, 1)), ('cp', 'dp'))
        dx_hat = dx_norm * norm_gain
        d_hidden = (inv_rms * (dx_hat - x_hat * jnp.mean(dx_hat * x_hat, axis=-1, keepdims=True))).astype(jnp.bfloat16)
        return tok_loss, loss_mean, d_hidden, d_gain, d_head

    return jax.shard_map(local_fn, mesh=mesh, in_specs=(P('dp', 'cp', None), P('dp', 'cp'), P('dp'), P(None), P(None, 'tp')), out_specs=(P('dp', 'cp'), P(), P('dp', 'cp', None), P(None), P(None, 'tp')), check_vma=False)
```

profile of v0, /device:TPU:1, one launch (start us, length us, event | category | flops | bytes accessed | tf_op | source)
XLA Modules:
  0.0 2642.3 jit_solution(12007238861405153974)
XLA Ops:
  7.2 0.0 all-reduce.5.cloned.1.call-start
  7.2 1.5 slice_reduce_fusion
  8.7 1.3 collective-permute-start
  10.0 5.1 collective-permute-start.1
  15.0 1.4 fusion.19
  16.5 1.3 add_reduce_fusion
  18.4 7.4 psum.52
  25.9 2.1 fusion.14
  27.9 3.5 fusion.25
  31.4 63.4 %fusion.20 = (f32[16,32]{1,0:T(8,128)S(1)}, f32[16,32,24576]{2,1,0:T(8,128)}) fusion(bf16[2048,24576]{1,0:T(8,128)(2,1)} %param.9, bf16[16,32,2048]{2,1,0:T(8,128)(2,1)} %param.5, f32[2048]{0:T(1024)} %param.8, f32[16,32]{1,0:T(8,128)S(1)} %add_rsqrt_fusion), kind=kOutput, calls=%fused_computation.38 | convolution fusion | flops 51556384768 | bytes 153104384 | tf_op jit(solution)/shard_map/bsd,dv->bsv/dot_general | solution.py:35
  94.8 3.8 pmax.7
  98.6 0.1 add_add_fusion
  99.3 0.0 collective-permute-done
  99.3 0.7 fusion.17
  100.0 0.1 copy.12
  100.1 0.0 collective-permute-done.1
  100.1 0.7 copy.13
  100.8 0.1 add_subtract_fusion
  100.9 23.7 select_reduce_fusion
  124.6 6.3 all-reduce.1
  130.8 1.3 fusion.18
  132.1 63.8 %fusion = f32[16,32,2048]{2,1,0:T(8,128)} fusion(bf16[2048,24576]{1,0:T(8,128)(2,1)} %param.9, f32[16,32,24576]{2,1,0:T(8,128)} %get-tuple-element.22, f32[16,32]{1,0:T(8,128)S(1)} %get-tuple-element.20, f32[16,32]{1,0:T(8,128)S(1)} %get-tuple-element.17, s32[16,32]{1,0:T(8,128)S(1)} %add_subtract_fusion), kind=kOutput, calls=%fused_computation.1 | convolution fusion | flops 51615105024 | bytes 155195392 | tf_op jit(solution)/shard_map/bsv,dv->bsd/dot_general | solution.py:49
  195.9 0.0 all-reduce.5.cloned.1.call-update
  195.9 0.0 all-reduce.7.cloned.1.call-start
  196.0 92.7 %convolution_bitcast_fusion = f32[2048,24576]{1,0:T(8,128)} fusion(f32[16,32,24576]{2,1,0:T(8,128)} %get-tuple-element.22, f32[16,32]{1,0:T(8,128)S(1)} %get-tuple-element.20, f32[16,32]{1,0:T(8,128)S(1)} %get-tuple-element.17, s32[16,32]{1,0:T(8,128)S(1)} %add_subtract_fusion, bf16[16,32,2048]{2,1,0:T(8,128)(2,1)S(1)} %copy-done.4), kind=kOutput, calls=%fused_computation | convolution fusion | flops 51615105024 | bytes 253761536 | tf_op jit(solution)/shard_map/bsd,bsv->dv/dot_general | solution.py:50
  288.7 0.0 all-reduce.7.cloned.1.call-update
  288.7 13.5 all-reduce.5.cloned.1.call-done
  302.2 3.4 fusion.13
  305.7 13.8 all-reduce
  320.7 4.5 fusion.12
  325.2 2180.9 %all-reduce.7.cloned.1.call-done = f32[2048,24576]{1,0:T(8,128)} async-done(((f32[2048,24576]{1,0:T(8,128)}), f32[2048,24576]{1,0:T(8,128)}) %all-reduce.7.cloned.1.call-update) | async-done | bytes 201326608 | tf_op jit(solution)/shard_map/psum | solution.py:50
  2506.1 128.3 %copy.16 = f32[2048,24576]{1,0:T(8,128)} copy(f32[2048,24576]{1,0:T(8,128)} %all-reduce.7.cloned.1.call-done) | data formatting | bytes 402653184
  (19 shorter events, 0.0 us)
Async XLA Ops:
  7.2 295.1 %all-reduce.5.cloned.1.call-start = ((), (), s32[]{:S(2)}) async-start(), calls=%async_computation | async-start | bytes 8388608 | tf_op jit(solution)/shard_map/psum | solution.py:49
  8.7 90.6 %collective-permute-start = (s32[16]{0:T(128)}, s32[16]{0:T(128)}, u32[]{:S(2)}, u32[]{:S(2)}) collective-permute-start(s32[16]{0:T(128)} %get-tuple-element.9), channel_id=1, source_target_pairs={{4,0},{5,1},{6,2},{7,3},{12,8},{13,9},{14,10},{15,11}} | collective-permute-start | bytes 200 | tf_op jit(solution)/shard_map/ppermute | solution.py:21
  10.0 90.1 %collective-permute-start.1 = (s32[16]{0:T(128)}, s32[16]{0:T(128)}, u32[]{:S(2)}, u32[]{:S(2)}) collective-permute-start(s32[16]{0:T(128)} %get-tuple-element.10), channel_id=1, source_target_pairs={{0,4},{1,5},{2,6},{3,7},{8,12},{9,13},{10,14},{11,15}} | collective-permute-start | bytes 200 | tf_op jit(solution)/shard_map/ppermute | solution.py:22
  27.9 66.9 %copy-start = (f32[16,32]{1,0:T(8,128)}, f32[16,32]{1,0:T(8,128)S(1)}, u32[]{:S(2)}) copy-start(f32[16,32]{1,0:T(8,128)S(1)} %add_rsqrt_fusion) | copy-start | bytes 6148
  31.4 69.4 %copy-start.5 = (s32[16,15]{1,0:T(8,128)S(1)}, s32[16,15]{1,0:T(8,128)}, u32[]{:S(2)}) copy-start(s32[16,15]{1,0:T(8,128)} %get-tuple-element.18) | copy-start | bytes 2884
  31.4 69.4 %copy-start.6 = (s32[16,15]{1,0:T(8,128)S(1)}, s32[16,15]{1,0:T(8,128)}, u32[]{:S(2)}) copy-start(s32[16,15]{1,0:T(8,128)} %get-tuple-element.19) | copy-start | bytes 2884
  100.9 30.0 %copy-start.7 = (s32[16]{0:T(128)S(1)}, s32[16]{0:T(128)}, u32[]{:S(2)}) copy-start(s32[16]{0:T(128)} %param.7) | copy-start | bytes 196
  132.1 63.9 %copy-start.4 = (bf16[16,32,2048]{2,1,0:T(8,128)(2,1)S(1)}, bf16[16,32,2048]{2,1,0:T(8,128)(2,1)}, u32[]{:S(2)}) copy-start(bf16[16,32,2048]{2,1,0:T(8,128)(2,1)} %fusion.25) | copy-start | bytes 6291460
  195.9 2310.1 %all-reduce.7.cloned.1.call-start = ((), (), s32[]{:S(2)}) async-start(), calls=%async_computation.1 | async-start | bytes 402653184 | tf_op jit(solution)/shard_map/psum | solution.py:50
  288.7 13.5 copy-start.1
  288.7 13.5 copy-start.2
  288.7 13.5 copy-start.3
Sparse Core Ops, SparseCore 0:
  196.1 106.1 all-reduce.4
  306.6 2199.4 all-reduce.6
where the time goes:
time: 2640 us
  waiting for transfers between devices  2190 us (83%)
  matrix products  220 us (8%)
  local copies, waits for them, and re-layouts  132 us (5%)
  other arithmetic  40.6 us (2%)
  blocking collectives  31.3 us (1%)
    psum x1, waiting for transfers between devices, local_fn(): lax.psum(jnp.einsum('bsd,bsv->dv', x_norm, d_logits, preferred_element_ty...  2180 us
    unnamed x17, local copies, waits for them, and re-layouts  128 us
    dot_general x1, matrix products, local_fn(): jnp.einsum('bsd,bsv->dv', x_norm, d_logits, preferred_element_type=jnp.fl...  92.7 us
    dot_general x1, matrix products, local_fn(): jnp.einsum('bsv,dv->bsd', d_logits, w_head, preferred_element_type=jnp.fl...  63.8 us
    dot_general x1, matrix products, local_fn(): jnp.einsum('bsd,dv->bsv', x_norm, w_head, preferred_element_type=jnp.floa...  63.4 us
  transfers between devices with their start and end apart: 4, of which 2 were waited for; matrix products, arithmetic and copies ran while one was open for 7% of the time, Pallas kernels for 0%

commit v1 on v0

v1 whole, which is shorter than its diff:
```python
import functools

import jax
import jax.numpy as jnp
import numpy as np
from jax import lax
from jax.experimental import pallas as pl
from jax.experimental.pallas import tpu as pltpu
from jax.sharding import PartitionSpec as P


NORM_EPS = 1e-5
BN = 512
N_CHUNK = 4
SHARED_SIZES = (3, 3)
COMMON_SIZES = (4, 4, 2, 2)
VMEM_LIMIT = 67043328


def logits_kernel(x_ref, w_ref, z_ref, m_ref, s_ref):
    @pl.when(pl.program_id(0) == 0)
    def _():
        m_ref[...] = jnp.full_like(m_ref, -jnp.inf)
        s_ref[...] = jnp.zeros_like(s_ref)

    sub = 512
    for j in range(w_ref.shape[1] // sub):
        z = jnp.dot(x_ref[...], w_ref[:, j * sub:(j + 1) * sub], preferred_element_type=jnp.float32)
        z_ref[:, j * sub:(j + 1) * sub] = z
        parts = [z[:, k * 128:(k + 1) * 128] for k in range(sub // 128)]
        m_old = m_ref[...]
        m_new = functools.reduce(jnp.maximum, parts, m_old)
        acc = s_ref[...] * jnp.exp(m_old - m_new)
        for part in parts:
            acc = acc + jnp.exp(part - m_new)
        s_ref[...] = acc
        m_ref[...] = m_new


def logits_pass(x_norm, w_head, block):
    rows, depth = x_norm.shape
    vocab = w_head.shape[1]
    return pl.pallas_call(
        logits_kernel,
        grid=(vocab // block,),
        in_specs=[pl.BlockSpec((rows, depth), lambda i: (0, 0)), pl.BlockSpec((depth, block), lambda i: (0, i))],
        out_specs=[pl.BlockSpec((rows, block), lambda i: (0, i)), pl.BlockSpec((rows, 128), lambda i: (0, 0)), pl.BlockSpec((rows, 128), lambda i: (0, 0))],
        out_shape=[jax.ShapeDtypeStruct((rows, vocab), jnp.float32), jax.ShapeDtypeStruct((rows, 128), jnp.float32), jax.ShapeDtypeStruct((rows, 128), jnp.float32)],
        compiler_params=pltpu.CompilerParams(vmem_limit_bytes=VMEM_LIMIT, dimension_semantics=('arbitrary',)),
        cost_estimate=pl.CostEstimate(flops=2 * rows * depth * vocab, bytes_accessed=vocab * (depth * 2 + rows * 4), transcendentals=rows * vocab),
        name='logits_pass',
    )(x_norm, w_head)


def dx_kernel(n_blocks, z_ref, w_ref, lse_ref, scale_ref, lab_ref, dx_ref, t_ref, dz_buf):
    i = pl.program_id(0)
    rows, block = z_ref.shape

    @pl.when(i == 0)
    def _():
        dx_ref[...] = jnp.zeros_like(dx_ref)
        t_ref[...] = jnp.zeros_like(t_ref)
        dz_buf[1] = jnp.zeros(dz_buf.shape[1:], dz_buf.dtype)

    now, before = lax.rem(i, 2), lax.rem(i + 1, 2)
    lse, scale, lab = lse_ref[...], scale_ref[...], lab_ref[...]
    lab = jnp.where(i < n_blocks, lab, -1)
    lane = lax.broadcasted_iota(jnp.int32, (rows, 128), 1)
    first = i * block
    n_sub = 4
    width = dx_ref.shape[1] // n_sub
    per_sub = block // 128 // n_sub
    hit_sum = t_ref[...]
    for j in range(n_sub):
        dz = dz_buf[before]
        dx_ref[:, j * width:(j + 1) * width] += lax.dot_general(dz, w_ref[j * width:(j + 1) * width, :], (((1,), (1,)), ((), ())), preferred_element_type=jnp.float32)
        for k in range(j * per_sub, (j + 1) * per_sub):
            z = z_ref[:, k * 128:(k + 1) * 128]
            hit = lab == lane + (first + k * 128)
            hit_sum = hit_sum + jnp.where(hit, z, 0.0)
            prob = jnp.exp(z - lse)
            dz_buf[now, :, k * 128:(k + 1) * 128] = (jnp.where(hit, prob - 1.0, prob) * scale).astype(jnp.bfloat16)
    t_ref[...] = hit_sum


def dx_pass(z, w_head, lse, scale, lab, block):
    rows, vocab = z.shape
    depth = w_head.shape[0]
    n_blocks = vocab // block
    row_spec = pl.BlockSpec((rows, 128), lambda i: (0, 0))
    return pl.pallas_call(
        functools.partial(dx_kernel, n_blocks),
        grid=(n_blocks + 1,),
        in_specs=[pl.BlockSpec((rows, block), lambda i: (0, jnp.minimum(i, n_blocks - 1))), pl.BlockSpec((depth, block), lambda i: (0, jnp.maximum(i - 1, 0))), row_spec, row_spec, row_spec],
        out_specs=[pl.BlockSpec((rows, depth), lambda i: (0, 0)), row_spec],
        out_shape=[jax.ShapeDtypeStruct((rows, depth), jnp.float32), jax.ShapeDtypeStruct((rows, 128), jnp.float32)],
        scratch_shapes=[pltpu.VMEM((2, rows, block), jnp.bfloat16)],
        compiler_params=pltpu.CompilerParams(vmem_limit_bytes=VMEM_LIMIT, dimension_semantics=('arbitrary',)),
        cost_estimate=pl.CostEstimate(flops=2 * rows * depth * vocab, bytes_accessed=vocab * (depth * 2 + rows * 4), transcendentals=rows * vocab),
        name='dx_pass',
    )(z, w_head, lse, scale, lab)


def prep_kernel(x_ref, g_ref, lse_ref, scale_ref, lab_ref, xn_ref, xt_ref, lse_out, scale_out, lab_out):
    xn = (x_ref[...] * g_ref[...]).astype(jnp.bfloat16)
    xn_ref[...] = xn
    xt_ref[...] = xn.T
    block = x_ref.shape[0]

    def wide(ref):
        return jnp.broadcast_to(ref[0], (128, block)).T

    lse_out[...] = wide(lse_ref)
    scale_out[...] = wide(scale_ref)
    lab_out[...] = wide(lab_ref).astype(jnp.int32)


def prep_pass(x_all, norm_gain, lse, scale, lab):
    tokens, depth = x_all.shape
    n, block = lse.shape
    row_spec = pl.BlockSpec((1, 1, block), lambda i: (i, 0, 0))
    wide_spec = pl.BlockSpec((block, 128), lambda i: (i, 0))
    return pl.pallas_call(
        prep_kernel,
        grid=(n,),
        in_specs=[pl.BlockSpec((block, depth), lambda i: (i, 0)), pl.BlockSpec((1, depth), lambda i: (0, 0)), row_spec, row_spec, row_spec],
        out_specs=[pl.BlockSpec((block, depth), lambda i: (i, 0)), pl.BlockSpec((depth, block), lambda i: (0, i)), wide_spec, wide_spec, wide_spec],
        out_shape=[jax.ShapeDtypeStruct((tokens, depth), jnp.bfloat16), jax.ShapeDtypeStruct((depth, tokens), jnp.bfloat16)] + [jax.ShapeDtypeStruct((tokens, 128), t) for t in (jnp.float32, jnp.float32, jnp.int32)],
        compiler_params=pltpu.CompilerParams(vmem_limit_bytes=VMEM_LIMIT, dimension_semantics=('arbitrary',)),
        cost_estimate=pl.CostEstimate(flops=8 * tokens * depth, bytes_accessed=8 * tokens * depth, transcendentals=0),
        name='prep_pass',
    )(x_all, norm_gain[None], lse[:, None], scale[:, None], lab[:, None])


def dw_kernel(n, halves, n_recv, lanes, has_prev, cols_ref, rcols_ref, w_ref, xn_hbm, xt_hbm, lse_hbm, scale_hbm, lab_hbm, *rest):
    recvs = rest[:n_recv]
    rest = rest[n_recv + (1 if has_prev else 0):]
    out_ref = rest[0]
    n_sends = 2 if halves else 1
    sends = rest[1:1 + n_sends]
    xn, xt, lse_v, scale_v, lab_v, dz_buf, o_buf, r_buf, in_sem, st_sem, out_sem, send_sem, rin_sem, rout_sem = rest[1 + n_sends:]
    i = pl.program_id(0)
    tokens, depth = xn.shape
    tok = tokens // N_CHUNK
    row = depth // N_CHUNK
    now, before = lax.rem(i, 2), lax.rem(i + 1, 2)

    def xn_copy(t):
        part = pl.ds(pl.multiple_of(t * tok, tok), tok)
        return pltpu.make_async_copy(xn_hbm.at[part, :], xn.at[part, :], in_sem.at[t])

    def xt_copy(t):
        part = pl.ds(pl.multiple_of(t * row, row), row)
        return pltpu.make_async_copy(xt_hbm.at[part, :], xt.at[part, :], in_sem.at[N_CHUNK + t])

    def stat_copies():
        return [pltpu.make_async_copy(src, dst, st_sem.at[k]) for k, (src, dst) in enumerate(((lse_hbm, lse_v), (scale_hbm, scale_v), (lab_hbm, lab_v)))]

    def tile(ref, r, block):
        return ref.at[pl.ds(pl.multiple_of(r * row, row), row), pl.ds(pl.multiple_of(block * BN, BN), BN)]

    def out_copy(step, t, slot):
        return pltpu.make_async_copy(o_buf.at[slot], tile(out_ref, t, cols_ref[step]), out_sem.at[slot])

    def send_copy(k, r, block, slot):
        return pltpu.make_async_copy(o_buf.at[slot], tile(sends[k], r, block), send_sem.at[slot])

    def finish_out(slot):
        out_copy(0, 0, slot).wait()
        send_copy(0, 0, 0, slot).wait()

    def rin_copy(lane, ref, r, block, slot):
        return pltpu.make_async_copy(tile(ref, r, block), r_buf.at[slot, lane], rin_sem.at[slot, lane])

    def rout_copy(lane, r, block, slot):
        return pltpu.make_async_copy(r_buf.at[slot, lane], tile(out_ref, r, block), rout_sem.at[slot, lane])

    def move_tiles(t):
        v = i * N_CHUNK + t
        slot, other = lax.rem(v, 2), lax.rem(v + 1, 2)
        for lane, entries in enumerate(lanes):
            total = sum(entry[4] for entry in entries)
            at = 0
            for k, first_col, first_row, u0, count, per_block in entries:
                @pl.when((v >= at + 1) & (v < at + 1 + count))
                def _(at=at, first_col=first_col, first_row=first_row, u0=u0, per_block=per_block):
                    u = v - 1 - at + u0
                    rin_copy(lane, recvs[0], 0, 0, other).wait()
                    rout_copy(lane, first_row + lax.rem(u, per_block), rcols_ref[first_col + u // per_block], other).start()

                at += count

            @pl.when((v >= 2) & (v < total + 2))
            def _():
                rout_copy(lane, 0, 0, slot).wait()

            at = 0
            for k, first_col, first_row, u0, count, per_block in entries:
                @pl.when((v >= at) & (v < at + count))
                def _(at=at, k=k, u0=u0, per_block=per_block):
                    u = v - at + u0
                    rin_copy(lane, recvs[k], lax.rem(u, per_block), u // per_block, slot).start()

                at += count

    def make_dz(t):
        part = pl.ds(pl.multiple_of(t * tok, tok), tok)
        z = jnp.dot(xn[part, :], w_ref[...], preferred_element_type=jnp.float32)
        lse, scale, lab = lse_v[part, :], scale_v[part, :], lab_v[part, :]
        lane_id = lax.broadcasted_iota(jnp.int32, (tok, 128), 1)
        first = cols_ref[jnp.minimum(i, n - 1)] * BN
        for k in range(BN // 128):
            prob = jnp.exp(z[:, k * 128:(k + 1) * 128] - lse)
            hit = lab == lane_id + (first + k * 128)
            dz_buf[now, part, k * 128:(k + 1) * 128] = (jnp.where(hit, prob - 1.0, prob) * scale).astype(jnp.bfloat16)

    def make_dw(t):
        part = pl.ds(pl.multiple_of(t * row, row), row)
        o_buf[lax.rem(t, 2)] = jnp.dot(xt[part, :], dz_buf[before], preferred_element_type=jnp.float32)

    def flush(t):
        slot = lax.rem(t, 2)
        out_copy(i - 1, t, slot).start()
        if halves:
            @pl.when(t < N_CHUNK // 2)
            def _():
                send_copy(0, t, i - 1, slot).start()

            @pl.when(t >= N_CHUNK // 2)
            def _():
                send_copy(1, t - N_CHUNK // 2, i - 1, slot).start()
        else:
            send_copy(0, t, i - 1, slot).start()

    def loop(do_dz, do_dw):
        def body(t, carry):
            move_tiles(t)
            if do_dw:
                @pl.when((i > 1) | (t > 1))
                def _():
                    finish_out(lax.rem(t, 2))

                @pl.when(i == 1)
                def _():
                    xt_copy(t).wait()
            else:
                xn_copy(t).wait()

                @pl.when(t + 2 < N_CHUNK)
                def _():
                    xn_copy(t + 2).start()

                xt_copy(t).start()
            if do_dz:
                make_dz(t)
            if do_dw:
                make_dw(t)
                flush(t)
            return carry

        lax.fori_loop(0, N_CHUNK, body, 0)

    @pl.when(i == 0)
    def _():
        xn_copy(0).start()
        for copy in stat_copies():
            copy.start()
        xn_copy(1).start()
        for copy in stat_copies():
            copy.wait()
        loop(True, False)

    @pl.when((i > 0) & (i < n))
    def _():
        loop(True, True)

    @pl.when(i == n)
    def _():
        loop(False, True)
        finish_out(0)
        finish_out(1)


def plan_lanes(recvs, row, n):
    room = (n + 1) * N_CHUNK - 2
    lanes, left, first_col = [], 0, 0
    for k, (array, first_row) in enumerate(recvs):
        per_block = array.shape[0] // row
        total = per_block * (array.shape[1] // BN)
        done = 0
        while done < total:
            if left == 0:
                lanes.append([])
                left = room
            take = min(left, total - done)
            lanes[-1].append((k, first_col, first_row, done, take, per_block))
            done += take
            left -= take
        first_col += array.shape[1] // BN
    return tuple(tuple(lane) for lane in lanes)


def dw_pass(cols, halves, recvs, rcols, prev, w_head, xn, xt, lse, scale, lab):
    n = cols.shape[0]
    depth, vocab = w_head.shape
    tokens = xn.shape[0]
    row = depth // N_CHUNK
    hbm = pl.BlockSpec(memory_space=pl.ANY)
    operands = [w_head, xn, xt, lse, scale, lab, *[r for r, _ in recvs]]
    if prev is not None:
        operands.append(prev)
    lanes = plan_lanes(recvs, row, n)
    n_lanes = max(len(lanes), 1)
    send_rows = [depth // 2] * 2 if halves else [depth]
    out_shape = [jax.ShapeDtypeStruct((depth, vocab), jnp.float32)] + [jax.ShapeDtypeStruct((r, n * BN), jnp.float32) for r in send_rows]
    grid_spec = pltpu.PrefetchScalarGridSpec(
        num_scalar_prefetch=2,
        grid=(n + 1,),
        in_specs=[pl.BlockSpec((depth, BN), lambda i, cols, rcols: (0, cols[jnp.minimum(i, n - 1)]))] + [hbm] * (len(operands) - 1),
        out_specs=[hbm] * len(out_shape),
        scratch_shapes=[
            pltpu.VMEM((tokens, depth), jnp.bfloat16),
            pltpu.VMEM((depth, tokens), jnp.bfloat16),
            pltpu.VMEM((tokens, 128), jnp.float32),
            pltpu.VMEM((tokens, 128), jnp.float32),
            pltpu.VMEM((tokens, 128), jnp.int32),
            pltpu.VMEM((2, tokens, BN), jnp.bfloat16),
            pltpu.VMEM((2, row, BN), jnp.float32),
            pltpu.VMEM((2, n_lanes, row, BN) if lanes else (2, 1, 8, 128), jnp.float32),
            pltpu.SemaphoreType.DMA((2 * N_CHUNK,)),
            pltpu.SemaphoreType.DMA((3,)),
            pltpu.SemaphoreType.DMA((2,)),
            pltpu.SemaphoreType.DMA((2,)),
            pltpu.SemaphoreType.DMA((2, n_lanes)),
            pltpu.SemaphoreType.DMA((2, n_lanes)),
        ],
    )
    width = n * BN
    return pl.pallas_call(
        functools.partial(dw_kernel, n, halves, len(recvs), lanes, prev is not None),
        grid_spec=grid_spec,
        out_shape=out_shape,
        input_output_aliases={} if prev is None else {2 + len(operands) - 1: 0},
        compiler_params=pltpu.CompilerParams(vmem_limit_bytes=VMEM_LIMIT, dimension_semantics=('arbitrary',)),
        cost_estimate=pl.CostEstimate(flops=4 * tokens * depth * width, bytes_accessed=depth * width * 10, transcendentals=tokens * width),
    )(cols, rcols, *operands)


def place_kernel(n_recv, starts, at_row, at_col, *refs):
    recvs, out_ref = refs[:n_recv], refs[n_recv + 1]
    i = pl.program_id(0)
    for k, ref in enumerate(recvs):
        @pl.when((i >= starts[k]) & (i < starts[k + 1]))
        def _(ref=ref):
            out_ref[...] = ref[...]


def place_pass(recvs, rcols, prev):
    depth = prev.shape[0]
    half = depth // 2
    steps, sizes, first_col = [], [], 0
    for array, first_row in recvs:
        per_block = array.shape[0] // half
        for block in range(array.shape[1] // BN):
            for r in range(per_block):
                steps.append((first_row // (N_CHUNK // 2) + r, first_col + block))
        first_col += array.shape[1] // BN
        sizes.append((per_block, per_block * (array.shape[1] // BN)))
    starts = [0] + [int(v) for v in np.cumsum([size for _, size in sizes])]
    at_row = jnp.asarray([r for r, _ in steps], jnp.int32)
    at_col = rcols[np.asarray([c for _, c in steps])]

    def recv_spec(k):
        per_block, size = sizes[k]

        def at(i, at_row, at_col):
            u = jnp.clip(i - starts[k], 0, size - 1)
            return lax.rem(u, per_block), lax.div(u, per_block)

        return pl.BlockSpec((half, BN), at)

    return pl.pallas_call(
        functools.partial(place_kernel, len(recvs), tuple(starts)),
        grid_spec=pltpu.PrefetchScalarGridSpec(
            num_scalar_prefetch=2,
            grid=(starts[-1],),
            in_specs=[recv_spec(k) for k in range(len(recvs))] + [pl.BlockSpec(memory_space=pl.ANY)],
            out_specs=pl.BlockSpec((half, BN), lambda i, at_row, at_col: (at_row[i], at_col[i])),
        ),
        out_shape=jax.ShapeDtypeStruct(prev.shape, prev.dtype),
        input_output_aliases={2 + len(recvs): 0},
        compiler_params=pltpu.CompilerParams(vmem_limit_bytes=VMEM_LIMIT, dimension_semantics=('arbitrary',)),
        cost_estimate=pl.CostEstimate(flops=half * BN * starts[-1], bytes_accessed=8 * half * BN * starts[-1], transcendentals=0),
        name='place_pass',
    )(at_row, at_col, *[r for r, _ in recvs], prev)


def solution(mesh):
    tp_size, cp_size, dp_size = mesh.shape['tp'], mesh.shape['cp'], mesh.shape['dp']
    from_next_pairs = [(cp_idx + 1, cp_idx) for cp_idx in range(cp_size - 1)]
    from_prev_pairs = [(cp_idx - 1, cp_idx) for cp_idx in range(1, cp_size)]
    tp_swap = [(t, 1 - t) for t in range(tp_size)]
    cp_swap = [(c, 1 - c) for c in range(cp_size)]
    core_swap = [(d, d ^ 1) for d in range(dp_size)]
    x_swap = [(d, d ^ 2) for d in range(dp_size)]

    def local_fn(hidden, tokens, seq_lens, norm_gain, w_head):
        n_seqs, local_len, depth = hidden.shape
        rows = n_seqs * local_len
        seg_len = local_len // 2
        vocab_local = w_head.shape[1]
        cp_rank = lax.axis_index('cp')
        tp_rank = lax.axis_index('tp')
        dp_rank = lax.axis_index('dp')
        core = dp_rank % 2

        def swap(v, axis, pairs):
            return lax.ppermute(v, axis, pairs)

        h_f32 = hidden.reshape(rows, depth).astype(jnp.float32)
        inv_rms = lax.rsqrt(jnp.mean(h_f32 * h_f32, axis=-1, keepdims=True) + NORM_EPS)
        x_hat = h_f32 * inv_rms
        x_norm = (x_hat * norm_gain).astype(jnp.bfloat16)
        x_all = lax.all_gather(x_hat, ('cp', 'dp'), tiled=True)

        next_first = lax.ppermute(tokens[:, 0], 'cp', from_next_pairs)
        prev_second = lax.ppermute(tokens[:, seg_len], 'cp', from_prev_pairs)
        first_end = jnp.where(cp_rank == cp_size - 1, tokens[:, seg_len], next_first)
        labels = jnp.concatenate([tokens[:, 1:seg_len], first_end[:, None], tokens[:, seg_len + 1:], prev_second[:, None]], axis=1)
        seg_pos = jnp.arange(seg_len)
        positions = jnp.concatenate([cp_rank * seg_len + seg_pos, (2 * cp_size - 1 - cp_rank) * seg_len + seg_pos])
        valid_mask = (positions[None, :] + 1 < seq_lens[:, None]).astype(jnp.float32)

        z, m_lane, s_lane = logits_pass(x_norm, w_head, 1024)
        m_loc = jnp.max(m_lane, axis=-1)
        s_loc = jnp.sum(s_lane * jnp.exp(m_lane - m_loc[:, None]), axis=-1)

        stats = jnp.stack([m_loc, s_loc, labels.reshape(rows).astype(jnp.float32), valid_mask.reshape(rows)])
        stats = lax.all_gather(stats, ('tp', 'cp', 'dp')).reshape(tp_size, cp_size * dp_size, 4, rows)
        glob_max = jnp.max(stats[:, :, 0], axis=0)
        log_norm_all = glob_max + jnp.log(jnp.sum(stats[:, :, 1] * jnp.exp(stats[:, :, 0] - glob_max), axis=0))
        valid_all = stats[0, :, 3]
        valid_count = jnp.sum(valid_all)
        scale_all = valid_all / valid_count
        lab_f32 = stats[0, :, 2] - (tp_rank * vocab_local).astype(jnp.float32)

        def wide(v):
            return jnp.broadcast_to(v.reshape(-1, 1), (v.size, 128))

        mine = cp_rank * dp_size + dp_rank

        def own(v):
            return lax.dynamic_index_in_dim(v, mine, axis=0, keepdims=False)

        log_norm = own(log_norm_all)
        dx_part, t_lane = dx_pass(z, w_head, wide(log_norm), wide(own(scale_all)), wide(own(lab_f32).astype(jnp.int32)), 1024)
        t_part = jnp.sum(t_lane, axis=-1)
        dx_part, x_all = lax.optimization_barrier((dx_part, x_all))
        xn_all, xt_all, lse_w, scale_w, lab_w = prep_pass(x_all, norm_gain, log_norm_all, scale_all, lab_f32)
        dx_norm = dx_part + swap(dx_part, 'tp', tp_swap)
        target_logit = t_part + swap(t_part, 'tp', tp_swap)
        tok_loss = (log_norm - target_logit).reshape(n_seqs, local_len) * valid_mask

        sums = jnp.concatenate([jnp.sum(dx_norm * x_hat, axis=0), jnp.full((128,), jnp.sum(tok_loss))])
        sums = sums + swap(sums, 'dp', core_swap)
        sums = sums + swap(sums, 'dp', x_swap)
        sums = sums + swap(sums, 'cp', cp_swap)
        d_gain = sums[:depth]
        loss_mean = sums[depth] / valid_count
        dx_hat = dx_norm * norm_gain
        d_hidden = (inv_rms * (dx_hat - x_hat * jnp.mean(dx_hat * x_hat, axis=-1, keepdims=True))).astype(jnp.bfloat16)

        n_blocks = vocab_local // BN
        shared, common = SHARED_SIZES, COMMON_SIZES
        n_shared, n_common = sum(shared), sum(common)
        assert 4 * n_shared + 2 * n_common == n_blocks
        role = (dp_rank // 2 + cp_rank) % 2

        def shared_cols(k, who, part):
            first = sum(shared[:k])
            return (who * 2 * n_shared + part * n_shared + first + jnp.arange(shared[k])).astype(jnp.int32)

        def common_cols(k, part):
            first = sum(common[:k])
            return (4 * n_shared + part * n_common + first + jnp.arange(common[k])).astype(jnp.int32)

        lower = N_CHUNK // 2
        out = None

        def run(cols, halves, arrived):
            recvs = [pair for pair, _ in arrived]
            rcols = jnp.concatenate([c for _, c in arrived]) if arrived else jnp.zeros((1,), jnp.int32)
            return dw_pass(cols, halves, recvs, rcols, out, w_head, xn_all, xt_all, lse_w, scale_w, lab_w)

        from_core, from_chip, passed_on, from_core_common = {}, {}, {}, {}

        def share(k, send_x, send_y):
            cols = shared_cols(k, role, 1 - core)
            from_core[k] = [((swap(send_x, 'dp', core_swap), 0), cols), ((swap(send_y, 'dp', core_swap), lower), cols)]
            cols = shared_cols(k, 1 - role, core)
            from_chip[k] = [((swap(send_x, 'dp', x_swap), 0), cols), ((swap(send_y, 'cp', cp_swap), lower), cols)]

        def pass_on(k):
            nonlocal out
            cols = shared_cols(k, 1 - role, 1 - core)
            (up, _), (low, _) = [pair for pair, _ in from_chip[k]]
            up, low, out = lax.optimization_barrier((up, low, out))
            from_chip[k] = [((up, 0), from_chip[k][0][1]), ((low, lower), from_chip[k][1][1])]
            passed_on[k] = [((swap(up, 'dp', core_swap), 0), cols), ((swap(low, 'dp', core_swap), lower), cols)]

        def share_common(k, send):
            from_core_common[k] = [((swap(send, 'dp', core_swap), 0), common_cols(k, 1 - core))]

        out, *sent = run(shared_cols(0, role, core), True, [])
        share(0, *sent)
        out, *sent = run(shared_cols(1, role, core), True, [])
        share(1, *sent)
        out, *sent = run(common_cols(0, core), False, from_core[0])
        share_common(0, *sent)
        pass_on(0)
        out, *sent = run(common_cols(1, core), False, from_core[1] + from_chip[0])
        share_common(1, *sent)
        out, *sent = run(common_cols(2, core), False, passed_on[0] + from_core_common[0])
        share_common(2, *sent)
        pass_on(1)
        out, *sent = run(common_cols(3, core), False, from_chip[1] + from_core_common[1])
        share_common(3, *sent)
        last = passed_on[1] + from_core_common[2] + from_core_common[3]
        d_head = place_pass([pair for pair, _ in last], jnp.concatenate([c for _, c in last]), out)
        return tok_loss, loss_mean, d_hidden.reshape(hidden.shape), d_gain, d_head

    return jax.shard_map(local_fn, mesh=mesh, in_specs=(P('dp', 'cp', None), P('dp', 'cp'), P('dp'), P(None), P(None, 'tp')), out_specs=(P('dp', 'cp'), P(), P('dp', 'cp', None), P(None), P(None, 'tp')), check_vma=False)
```

time: 2640 us -> 947 us (0.36)
  waiting for transfers between devices: 2190 us -> 205 us
  Pallas kernels: 0 us -> 640 us
  matrix products: 220 us -> 0 us
  local copies, waits for them, and re-layouts: 132 us -> 11.4 us
    psum x2 -> x0, waiting for transfers between devices: 2190 us -> none  [the longest x1 2180 us: local_fn(): lax.psum(jnp.einsum('bsd,bsv->dv', x_norm, d_logits, preferred_element_ty...]
    pallas_call x0 -> x10, Pallas kernels: none -> 640 us  [the longest x6 438 us: dw_pass(): pl.pallas_call(functools.partial(dw_kernel, n, halves, len(recvs), lanes,...]
    dot_general x3 -> x0, matrix products: 220 us -> none  [the longest x1 92.7 us: local_fn(): jnp.einsum('bsd,bsv->dv', x_norm, d_logits, preferred_element_type=jnp.fl...]
    ppermute x0 -> x21, waiting for transfers between devices: none -> 205 us  [swap(): return lax.ppermute(v, axis, pairs)]
    unnamed x17 -> x26, local copies, waits for them, and re-layouts: 128 us -> 1.3 us
    psum x3 -> x0, blocking collectives: 27.5 us -> none  [the longest x1 13.8 us: local_fn(): loss_mean = lax.psum(jnp.sum(tok_loss), ('cp', 'dp')) / valid_count]
  transfers between devices with their start and end apart: 4 -> 24, of which waited for: 2 -> 8; matrix products, arithmetic and copies ran while one was open for 7% -> 4% of each run, Pallas kernels for 0% -> 49%
where the time goes in v1:
time: 947 us; the launch traced here: 939 us
  Pallas kernels  640 us (68%)
  waiting for transfers between devices  205 us (22%)
  other arithmetic  33.2 us (4%)
  between operations  17.3 us (2%)
  blocking collectives  16.6 us (2%)
  starting transfers between devices  15.6 us (2%)
  local copies, waits for them, and re-layouts  11.4 us (1%)
    pallas_call x6, Pallas kernels, dw_pass(): pl.pallas_call(functools.partial(dw_kernel, n, halves, len(recvs), lanes,...  438 us
    ppermute x21, waiting for transfers between devices, swap(): return lax.ppermute(v, axis, pairs)  205 us
    pallas_call x1, Pallas kernels, dx_pass(): pl.pallas_call(functools.partial(dx_kernel, n_blocks), grid=(n_blocks + 1...  77.3 us
    pallas_call x1, Pallas kernels, logits_pass(): pl.pallas_call(logits_kernel, grid=(vocab // block,), in_specs=[pl.BlockS...  72.7 us
    pallas_call x1, Pallas kernels, place_pass(): pl.pallas_call(functools.partial(place_kernel, len(recvs), tuple(starts))...  26.2 us
    pallas_call x1, Pallas kernels, prep_pass(): pl.pallas_call(prep_kernel, grid=(n,), in_specs=[pl.BlockSpec((block, dep...  26.1 us
  transfers between devices with their start and end apart: 24, of which 8 were waited for; matrix products, arithmetic and copies ran while one was open for 4% of the time, Pallas kernels for 49%

profile of v1, /device:TPU:1, one launch (start us, length us, event | category | flops | bytes accessed | tf_op | source)
XLA Modules:
  0.0 939.4 jit_solution(15518532803517168430)
XLA Ops:
  7.2 2.1 multiply_reduce_fusion.2
  9.4 4.9 bitcast_multiply_fusion
  15.6 1.3 collective-permute-start
  16.9 5.1 collective-permute-start.1
  23.4 72.7 %logits_pass.1 = (f32[512,24576]{1,0:T(8,128)}, f32[512,128]{1,0:T(8,128)}, f32[512,128]{1,0:T(8,128)}) custom-call(bf16[512,2048]{1,0:T(8,128)(2,1)} %get-tuple-element.76.x_ref, bf16[2048,24576]{1,0:T(8,128)(2,1)} %w_ref.15), custom_call_target="tpu_custom_call" | custom-call | flops 51539607552 | bytes 150994944 | tf_op jit(solution)/shard_map/logits_pass/pallas_call | solution.py:43
  96.0 1.1 reduce_max.18
  97.7 1.3 multiply_reduce_fusion.3
  102.2 16.6 %all-gather.1 = f32[16,4,512]{2,1,0:T(4,128)S(1)} all-gather(f32[1,4,512]{2,1,0:T(4,128)S(1)} %maximum_bitcast_fusion), channel_id=2, replica_groups=mesh['tp'=2,'cp'=2,'dp'=4] {'tp','cp','dp'}, dimensions={0}, use_global_device_ids=true | all-gather | bytes 139264 | tf_op jit(solution)/shard_map/all_gather | solution.py:439
  124.0 77.3 %dx_pass.1 = (f32[512,2048]{1,0:T(8,128)}, f32[512,128]{1,0:T(8,128)}) custom-call(f32[512,24576]{1,0:T(8,128)} %get-tuple-element.39.z_ref, bf16[2048,24576]{1,0:T(8,128)(2,1)} %w_ref.15, f32[512,128]{1,0:T(8,128)} %broadcast_in_dim.18.lse_ref, f32[512,128]{1,0:T(8,128)} %broadcast_in_dim.20.scale_ref, s32[512,128]{1,0:T(8,128)} %broadcast_in_dim.21.lab_ref), custom_call_target="tpu_custom_call" | custom-call | flops 51539607552 | bytes 150994944 | tf_op jit(solution)/shard_map/dx_pass/pallas_call | solution.py:91
  201.3 26.1 %prep_pass.1 = (bf16[4096,2048]{1,0:T(8,128)(2,1)}, bf16[2048,4096]{1,0:T(8,128)(2,1)}, f32[4096,128]{1,0:T(8,128)}, f32[4096,128]{1,0:T(8,128)}, s32[4096,128]{1,0:T(8,128)}) custom-call(f32[4096,2048]{1,0:T(8,128)} %all-gather.4.cloned.1.call-done.x_ref, f32[1,2048]{1,0:T(1,128)} %bitcast.42, f32[8,1,512]{2,1,0:T(1,128)} %add.292.lse_ref, ...), custom_call_target="tpu_custom_call" | custom-call | flops 67108864 | bytes 67108864 | tf_op jit(solution)/shard_map/prep_pass/pallas_call | solution.py:123
  227.3 70.1 %shard_map.119 = (f32[2048,24576]{1,0:T(8,128)}, f32[1024,1536]{1,0:T(8,128)}, f32[1024,1536]{1,0:T(8,128)}) custom-call(s32[3]{0:T(128)} %iota_add_fusion.11.cols_ref, s32[1]{0:T(128)} %constant.98.clone.1.rcols_ref, bf16[2048,24576]{1,0:T(8,128)(2,1)} %w_ref.15, bf16[4096,2048]{1,0:T(8,128)(2,1)} %get-tuple-element.44.xn_hbm, ...), custom_call_target="tpu_custom_call" | custom-call | flops 51539607552 | bytes 31457280 | tf_op jit(solution)/shard_map/pallas_call | solution.py:339
  301.3 1.0 collective-permute-start.9
  302.3 70.2 %shard_map.120 = (f32[2048,24576]{1,0:T(8,128)}, f32[1024,1536]{1,0:T(8,128)}, f32[1024,1536]{1,0:T(8,128)}) custom-call(s32[3]{0:T(128)} %iota_add_fusion.12.cols_ref, s32[1]{0:T(128)} %constant.98.clone.1.rcols_ref, bf16[2048,24576]{1,0:T(8,128)(2,1)} %w_ref.15, bf16[4096,2048]{1,0:T(8,128)(2,1)} %get-tuple-element.44.xn_hbm, ...), custom_call_target="tpu_custom_call", output_to_operand_aliasing={{0}: (8, {})} | custom-call | flops 51539607552 | bytes 31457280 | tf_op jit(solution)/shard_map/pallas_call | solution.py:339
  373.3 94.0 %shard_map.121 = (f32[2048,24576]{1,0:T(8,128)}, f32[2048,2048]{1,0:T(8,128)}) custom-call(s32[4]{0:T(128)} %iota_add_fusion.7.cols_ref, s32[6]{0:T(128)} %pad_add_fusion.3.rcols_ref, bf16[2048,24576]{1,0:T(8,128)(2,1)} %w_ref.15, bf16[4096,2048]{1,0:T(8,128)(2,1)} %get-tuple-element.44.xn_hbm, ...), custom_call_target="tpu_custom_call", output_to_operand_aliasing={{0}: (10, {})} | custom-call | flops 68719476736 | bytes 41943040 | tf_op jit(solution)/shard_map/pallas_call | solution.py:339
  467.8 94.8 %shard_map.122 = (f32[2048,24576]{1,0:T(8,128)}, f32[2048,2048]{1,0:T(8,128)}) custom-call(s32[4]{0:T(128)} %iota_add_fusion.5.cols_ref, s32[12]{0:T(128)} %pad_add_fusion.4.rcols_ref, bf16[2048,24576]{1,0:T(8,128)(2,1)} %w_ref.15, bf16[4096,2048]{1,0:T(8,128)(2,1)} %get-tuple-element.44.xn_hbm, ...), custom_call_target="tpu_custom_call", output_to_operand_aliasing={{0}: (12, {})} | custom-call | flops 68719476736 | bytes 41943040 | tf_op jit(solution)/shard_map/pallas_call | solution.py:339
  563.8 33.3 %collective-permute-done.13.rest_0_ = f32[1024,1536]{1,0:T(8,128)} collective-permute-done((f32[1024,1536]{1,0:T(8,128)}, f32[1024,1536]{1,0:T(8,128)}, u32[]{:S(2)}, u32[]{:S(2)}) %collective-permute-start.13) | collective-permute-done | bytes 6291488 | tf_op jit(solution)/shard_map/ppermute | solution.py:418
  599.6 6.6 collective-permute-done.14.rest_1_
  606.2 54.6 %shard_map.123 = (f32[2048,24576]{1,0:T(8,128)}, f32[2048,1024]{1,0:T(8,128)}) custom-call(s32[2]{0:T(128)} %iota_add_fusion.10.cols_ref, s32[10]{0:T(128)} %pad_add_fusion.2.rcols_ref, bf16[2048,24576]{1,0:T(8,128)(2,1)} %w_ref.15, bf16[4096,2048]{1,0:T(8,128)(2,1)} %get-tuple-element.44.xn_hbm, ...), custom_call_target="tpu_custom_call", output_to_operand_aliasing={{0}: (11, {})} | custom-call | flops 34359738368 | bytes 20971520 | tf_op jit(solution)/shard_map/pallas_call | solution.py:339
  660.7 39.5 %collective-permute-done.7.rest_0_ = f32[1024,1536]{1,0:T(8,128)} collective-permute-done((f32[1024,1536]{1,0:T(8,128)}, f32[1024,1536]{1,0:T(8,128)}, u32[]{:S(2)}, u32[]{:S(2)}) %collective-permute-start.7) | collective-permute-done | bytes 6291488 | tf_op jit(solution)/shard_map/ppermute | solution.py:418
  700.2 34.2 %collective-permute-done.8.rest_1_ = f32[1024,1536]{1,0:T(8,128)} collective-permute-done((f32[1024,1536]{1,0:T(8,128)}, f32[1024,1536]{1,0:T(8,128)}, u32[]{:S(2)}, u32[]{:S(2)}) %collective-permute-start.8) | collective-permute-done | bytes 6291488 | tf_op jit(solution)/shard_map/ppermute | solution.py:418
  734.4 54.6 %shard_map.124 = (f32[2048,24576]{1,0:T(8,128)}, f32[2048,1024]{1,0:T(8,128)}) custom-call(s32[2]{0:T(128)} %iota_add_fusion.2.cols_ref, s32[10]{0:T(128)} %pad_add_fusion.5.rcols_ref, bf16[2048,24576]{1,0:T(8,128)(2,1)} %w_ref.15, bf16[4096,2048]{1,0:T(8,128)(2,1)} %get-tuple-element.44.xn_hbm, ...), custom_call_target="tpu_custom_call", output_to_operand_aliasing={{0}: (11, {})} | custom-call | flops 34359738368 | bytes 20971520 | tf_op jit(solution)/shard_map/pallas_call | solution.py:339
  789.1 1.0 collective-permute-start.22
  790.6 1.1 reduce_sum.76
  791.8 2.4 collective-permute-done.2
  795.7 1.2 gather_fusion
  796.9 1.3 select_reduce_fusion
  798.3 86.7 %collective-permute-done.3 = f32[512,2048]{1,0:T(8,128)} collective-permute-done((f32[512,2048]{1,0:T(8,128)}, f32[512,2048]{1,0:T(8,128)}, u32[]{:S(2)}, u32[]{:S(2)}) %collective-permute-start.3) | collective-permute-done | bytes 4194336 | tf_op jit(solution)/shard_map/ppermute | solution.py:418
  885.0 5.3 multiply_reduce_fusion
  891.1 2.5 collective-permute-start.4
  895.7 2.0 collective-permute-done.5
  897.7 4.6 multiply_convert_fusion
  904.7 26.2 %place_pass.1 = f32[2048,24576]{1,0:T(8,128)} custom-call(s32[14]{0:T(128)} %constant.101.clone.at_row, s32[14]{0:T(128)} %gather_fusion, f32[1024,1536]{1,0:T(8,128)} %collective-permute-done.18.refs_0_, f32[1024,1536]{1,0:T(8,128)} %collective-permute-done.19.refs_1_, ...), custom_call_target="tpu_custom_call", output_to_operand_aliasing={{}: (6, {})} | custom-call | flops 7340032 | bytes 58720256 | tf_op jit(solution)/shard_map/place_pass/pallas_call | solution.py:382
  (119 shorter events, 26.6 us)
Async XLA Ops:
  7.2 194.1 %all-gather.4.cloned.1.call-start = ((), (), s32[]{:S(2)}) async-start(), calls=%async_computation | async-start | bytes 37748736 | tf_op jit(solution)/shard_map/all_gather | solution.py:424
  9.4 4.9 copy-start.6
  14.2 7.8 copy-start.9
  15.6 84.3 %collective-permute-start = (s32[16]{0:T(128)}, s32[16]{0:T(128)}, u32[]{:S(2)}, u32[]{:S(2)}) collective-permute-start(s32[16]{0:T(128)} %get-tuple-element.71), channel_id=1, source_target_pairs={{4,0},{5,1},{6,2},{7,3},{12,8},{13,9},{14,10},{15,11}} | collective-permute-start | bytes 200 | tf_op jit(solution)/shard_map/ppermute | solution.py:426
  16.9 83.7 %collective-permute-start.1 = (s32[16]{0:T(128)}, s32[16]{0:T(128)}, u32[]{:S(2)}, u32[]{:S(2)}) collective-permute-start(s32[16]{0:T(128)} %get-tuple-element.72), channel_id=1, source_target_pairs={{0,4},{1,5},{2,6},{3,7},{8,12},{9,13},{10,14},{11,15}} | collective-permute-start | bytes 200 | tf_op jit(solution)/shard_map/ppermute | solution.py:427
  297.4 75.8 %collective-permute-start.11 = (f32[1024,1536]{1,0:T(8,128)}, f32[1024,1536]{1,0:T(8,128)}, u32[]{:S(2)}, u32[]{:S(2)}) collective-permute-start(f32[1024,1536]{1,0:T(8,128)} %get-tuple-element.52), channel_id=1, source_target_pairs={{0,1},{1,0},{2,3},{3,2},{4,5},{5,4},{6,7},{7,6},{8,9},{9,8},{10,11... | collective-permute-start | bytes 18874376 | tf_op jit(solution)/shard_map/ppermute | solution.py:418
  297.5 75.8 %collective-permute-start.12 = (f32[1024,1536]{1,0:T(8,128)}, f32[1024,1536]{1,0:T(8,128)}, u32[]{:S(2)}, u32[]{:S(2)}) collective-permute-start(f32[1024,1536]{1,0:T(8,128)} %get-tuple-element.53), channel_id=1, source_target_pairs={{0,1},{1,0},{2,3},{3,2},{4,5},{5,4},{6,7},{7,6},{8,9},{9,8},{10,11... | collective-permute-start | bytes 18874376 | tf_op jit(solution)/shard_map/ppermute | solution.py:418
  300.9 166.4 %collective-permute-start.10 = (f32[1024,1536]{1,0:T(8,128)}, f32[1024,1536]{1,0:T(8,128)}, u32[]{:S(2)}, u32[]{:S(2)}) collective-permute-start(f32[1024,1536]{1,0:T(8,128)} %get-tuple-element.53), channel_id=1, source_target_pairs={{0,4},{4,0},{1,5},{5,1},{2,6},{6,2},{3,7},{7,3},{8,12},{12,8},{9,1... | collective-permute-start | bytes 18874376 | tf_op jit(solution)/shard_map/ppermute | solution.py:418
  301.3 166.0 %collective-permute-start.9 = (f32[1024,1536]{1,0:T(8,128)}, f32[1024,1536]{1,0:T(8,128)}, u32[]{:S(2)}, u32[]{:S(2)}) collective-permute-start(f32[1024,1536]{1,0:T(8,128)} %get-tuple-element.52), channel_id=1, source_target_pairs={{0,2},{1,3},{2,0},{3,1},{4,6},{5,7},{6,4},{7,5},{8,10},{9,11},{10,... | collective-permute-start | bytes 18874376 | tf_op jit(solution)/shard_map/ppermute | solution.py:418
  372.6 95.2 %collective-permute-start.16 = (f32[1024,1536]{1,0:T(8,128)}, f32[1024,1536]{1,0:T(8,128)}, u32[]{:S(2)}, u32[]{:S(2)}) collective-permute-start(f32[1024,1536]{1,0:T(8,128)} %get-tuple-element.50), channel_id=1, source_target_pairs={{0,1},{1,0},{2,3},{3,2},{4,5},{5,4},{6,7},{7,6},{8,9},{9,8},{10,11... | collective-permute-start | bytes 18874376 | tf_op jit(solution)/shard_map/ppermute | solution.py:418
  373.2 94.6 %collective-permute-start.17 = (f32[1024,1536]{1,0:T(8,128)}, f32[1024,1536]{1,0:T(8,128)}, u32[]{:S(2)}, u32[]{:S(2)}) collective-permute-start(f32[1024,1536]{1,0:T(8,128)} %get-tuple-element.51), channel_id=1, source_target_pairs={{0,1},{1,0},{2,3},{3,2},{4,5},{5,4},{6,7},{7,6},{8,9},{9,8},{10,11... | collective-permute-start | bytes 18874376 | tf_op jit(solution)/shard_map/ppermute | solution.py:418
  467.3 138.9 %collective-permute-start.15 = (f32[2048,2048]{1,0:T(8,128)}, f32[2048,2048]{1,0:T(8,128)}, u32[]{:S(2)}, u32[]{:S(2)}) collective-permute-start(f32[2048,2048]{1,0:T(8,128)} %get-tuple-element.58), channel_id=1, source_target_pairs={{0,1},{1,0},{2,3},{3,2},{4,5},{5,4},{6,7},{7,6},{8,9},{9,8},{10,11... | collective-permute-start | bytes 50331656 | tf_op jit(solution)/shard_map/ppermute | solution.py:418
  562.7 171.8 %collective-permute-start.21 = (f32[2048,2048]{1,0:T(8,128)}, f32[2048,2048]{1,0:T(8,128)}, u32[]{:S(2)}, u32[]{:S(2)}) collective-permute-start(f32[2048,2048]{1,0:T(8,128)} %get-tuple-element.65), channel_id=1, source_target_pairs={{0,1},{1,0},{2,3},{3,2},{4,5},{5,4},{6,7},{7,6},{8,9},{9,8},{10,11... | collective-permute-start | bytes 50331656 | tf_op jit(solution)/shard_map/ppermute | solution.py:418
  562.8 34.4 %collective-permute-start.13 = (f32[1024,1536]{1,0:T(8,128)}, f32[1024,1536]{1,0:T(8,128)}, u32[]{:S(2)}, u32[]{:S(2)}) collective-permute-start(f32[1024,1536]{1,0:T(8,128)} %collective-permute-done.9.rest_2_), channel_id=1, source_target_pairs={{0,1},{1,0},{2,3},{3,2},{4,5},{5,4},{6,7},{7,6},{8,9},{9,8},{10,11... | collective-permute-start | bytes 18874376 | tf_op jit(solution)/shard_map/ppermute | solution.py:418
  563.2 43.0 %collective-permute-start.14 = (f32[1024,1536]{1,0:T(8,128)}, f32[1024,1536]{1,0:T(8,128)}, u32[]{:S(2)}, u32[]{:S(2)}) collective-permute-start(f32[1024,1536]{1,0:T(8,128)} %collective-permute-done.10.rest_3_), channel_id=1, source_target_pairs={{0,1},{1,0},{2,3},{3,2},{4,5},{5,4},{6,7},{7,6},{8,9},{9,8},{10,11... | collective-permute-start | bytes 18874376 | tf_op jit(solution)/shard_map/ppermute | solution.py:418
  563.3 136.9 %collective-permute-start.7 = (f32[1024,1536]{1,0:T(8,128)}, f32[1024,1536]{1,0:T(8,128)}, u32[]{:S(2)}, u32[]{:S(2)}) collective-permute-start(f32[1024,1536]{1,0:T(8,128)} %get-tuple-element.50), channel_id=1, source_target_pairs={{0,2},{1,3},{2,0},{3,1},{4,6},{5,7},{6,4},{7,5},{8,10},{9,11},{10,... | collective-permute-start | bytes 18874376 | tf_op jit(solution)/shard_map/ppermute | solution.py:418
  597.2 137.3 %collective-permute-start.8 = (f32[1024,1536]{1,0:T(8,128)}, f32[1024,1536]{1,0:T(8,128)}, u32[]{:S(2)}, u32[]{:S(2)}) collective-permute-start(f32[1024,1536]{1,0:T(8,128)} %get-tuple-element.51), channel_id=1, source_target_pairs={{0,4},{4,0},{1,5},{5,1},{2,6},{6,2},{3,7},{7,3},{8,12},{12,8},{9,1... | collective-permute-start | bytes 18874376 | tf_op jit(solution)/shard_map/ppermute | solution.py:418
  789.1 115.6 %collective-permute-start.22 = (f32[2048,1024]{1,0:T(8,128)}, f32[2048,1024]{1,0:T(8,128)}, u32[]{:S(2)}, u32[]{:S(2)}) collective-permute-start(f32[2048,1024]{1,0:T(8,128)} %get-tuple-element.67), channel_id=1, source_target_pairs={{0,1},{1,0},{2,3},{3,2},{4,5},{5,4},{6,7},{7,6},{8,9},{9,8},{10,11... | collective-permute-start | bytes 25165832 | tf_op jit(solution)/shard_map/ppermute | solution.py:418
  790.1 114.6 %collective-permute-start.20 = (f32[2048,1024]{1,0:T(8,128)}, f32[2048,1024]{1,0:T(8,128)}, u32[]{:S(2)}, u32[]{:S(2)}) collective-permute-start(f32[2048,1024]{1,0:T(8,128)} %get-tuple-element.64), channel_id=1, source_target_pairs={{0,1},{1,0},{2,3},{3,2},{4,5},{5,4},{6,7},{7,6},{8,9},{9,8},{10,11... | collective-permute-start | bytes 25165832 | tf_op jit(solution)/shard_map/ppermute | solution.py:418
  790.1 114.5 %collective-permute-start.18 = (f32[1024,1536]{1,0:T(8,128)}, f32[1024,1536]{1,0:T(8,128)}, u32[]{:S(2)}, u32[]{:S(2)}) collective-permute-start(f32[1024,1536]{1,0:T(8,128)} %collective-permute-done.7.rest_0_), channel_id=1, source_target_pairs={{0,1},{1,0},{2,3},{3,2},{4,5},{5,4},{6,7},{7,6},{8,9},{9,8},{10,11... | collective-permute-start | bytes 18874376 | tf_op jit(solution)/shard_map/ppermute | solution.py:418
  790.6 114.1 %collective-permute-start.19 = (f32[1024,1536]{1,0:T(8,128)}, f32[1024,1536]{1,0:T(8,128)}, u32[]{:S(2)}, u32[]{:S(2)}) collective-permute-start(f32[1024,1536]{1,0:T(8,128)} %collective-permute-done.8.rest_1_), channel_id=1, source_target_pairs={{0,1},{1,0},{2,3},{3,2},{4,5},{5,4},{6,7},{7,6},{8,9},{9,8},{10,11... | collective-permute-start | bytes 18874376 | tf_op jit(solution)/shard_map/ppermute | solution.py:418
  791.7 2.5 collective-permute-start.2
  794.2 90.8 %collective-permute-start.3 = (f32[512,2048]{1,0:T(8,128)}, f32[512,2048]{1,0:T(8,128)}, u32[]{:S(2)}, u32[]{:S(2)}) collective-permute-start(f32[512,2048]{1,0:T(8,128)} %get-tuple-element.42), channel_id=1, source_target_pairs={{0,8},{8,0},{1,9},{9,1},{2,10},{10,2},{3,11},{11,3},{4,12},{12,4},... | collective-permute-start | bytes 12582920 | tf_op jit(solution)/shard_map/ppermute | solution.py:418
  798.3 95.3 %copy-start.10 = (s32[16]{0:T(128)S(1)}, s32[16]{0:T(128)}, u32[]{:S(2)}) copy-start(s32[16]{0:T(128)} %param.10) | copy-start | bytes 196
  798.3 95.3 %copy-start.12 = (s32[32]{0:T(128)S(1)}, s32[32]{0:T(128)}, u32[]{:S(2)}) copy-start(s32[32]{0:T(128)} %copy-done.11) | copy-start | bytes 388
  798.3 99.4 %copy-start = (bf16[16,32,2048]{2,1,0:T(8,128)(2,1)S(1)}, bf16[16,32,2048]{2,1,0:T(8,128)(2,1)}, u32[]{:S(2)}) copy-start(bf16[16,32,2048]{2,1,0:T(8,128)(2,1)} %param.8) | copy-start | bytes 6291460
  798.3 99.4 %copy-start.1 = (f32[512,2048]{1,0:T(8,128)S(1)}, f32[512,2048]{1,0:T(8,128)}, u32[]{:S(2)}) copy-start(f32[512,2048]{1,0:T(8,128)} %get-tuple-element.42) | copy-start | bytes 12582916
  798.3 99.4 %copy-start.3 = (f32[2048]{0:T(1024)S(1)}, f32[2048]{0:T(1024)}, u32[]{:S(2)}) copy-start(f32[2048]{0:T(1024)} %param.11) | copy-start | bytes 24580
  798.3 99.3 %copy-start.7 = (f32[512]{0:T(512)S(1)}, f32[512]{0:T(512)}, u32[]{:S(2)}) copy-start(f32[512]{0:T(512)} %copy-done.6) | copy-start | bytes 6148
  891.1 3.3 collective-permute-start.4
  895.0 2.6 collective-permute-start.5
  897.6 4.6 collective-permute-start.6
  (5 other events, 5.2 us)
Sparse Core Ops, SparseCore 0:
  14.4 159.6 all-gather.3

commit v2 on v1

--- a/solution.py
+++ b/solution.py
@@ -12,8 +12,8 @@
 NORM_EPS = 1e-5
 BN = 512
 N_CHUNK = 4
-SHARED_SIZES = (3, 3)
-COMMON_SIZES = (4, 4, 2, 2)
+SHARED_SIZES = (2, 4)
+COMMON_SIZES = (5, 4, 3)
 VMEM_LIMIT = 67043328
 
 
@@ -101,38 +101,46 @@
     )(z, w_head, lse, scale, lab)
 
 
-def prep_kernel(x_ref, g_ref, lse_ref, scale_ref, lab_ref, xn_ref, xt_ref, lse_out, scale_out, lab_out):
+def prep_kernel(mine_ref, x_ref, g_ref, *refs):
+    xn_ref, xt_ref, lse_out, scale_out, lab_out = refs[-5:]
+    source = jnp.bitwise_xor(mine_ref[0], pl.program_id(0))
+    stats = refs[0][...]
+    for k in range(1, len(refs) - 5):
+        stats = jnp.where(source == k, refs[k][...], stats)
     xn = (x_ref[...] * g_ref[...]).astype(jnp.bfloat16)
     xn_ref[...] = xn
     xt_ref[...] = xn.T
     block = x_ref.shape[0]
 
-    def wide(ref):
-        return jnp.broadcast_to(ref[0], (128, block)).T
-
-    lse_out[...] = wide(lse_ref)
-    scale_out[...] = wide(scale_ref)
-    lab_out[...] = wide(lab_ref).astype(jnp.int32)
-
-
-def prep_pass(x_all, norm_gain, lse, scale, lab):
+    def wide(k):
+        return jnp.broadcast_to(stats[k:k + 1, :], (128, block)).T
+
+    lse_out[...] = wide(0)
+    scale_out[...] = wide(2)
+    lab_out[...] = wide(1).astype(jnp.int32)
+
+
+def prep_pass(mine, x_all, norm_gain, stats):
     tokens, depth = x_all.shape
-    n, block = lse.shape
-    row_spec = pl.BlockSpec((1, 1, block), lambda i: (i, 0, 0))
-    wide_spec = pl.BlockSpec((block, 128), lambda i: (i, 0))
+    n = len(stats)
+    n_stats, block = stats[0].shape
+    wide_spec = pl.BlockSpec((block, 128), lambda i, mine: (i, 0))
     return pl.pallas_call(
         prep_kernel,
-        grid=(n,),
-        in_specs=[pl.BlockSpec((block, depth), lambda i: (i, 0)), pl.BlockSpec((1, depth), lambda i: (0, 0)), row_spec, row_spec, row_spec],
-        out_specs=[pl.BlockSpec((block, depth), lambda i: (i, 0)), pl.BlockSpec((depth, block), lambda i: (0, i)), wide_spec, wide_spec, wide_spec],
+        grid_spec=pltpu.PrefetchScalarGridSpec(
+            num_scalar_prefetch=1,
+            grid=(n,),
+            in_specs=[pl.BlockSpec((block, depth), lambda i, mine: (i, 0)), pl.BlockSpec((1, depth), lambda i, mine: (0, 0)), *[pl.BlockSpec((n_stats, block), lambda i, mine: (0, 0))] * n],
+            out_specs=[pl.BlockSpec((block, depth), lambda i, mine: (i, 0)), pl.BlockSpec((depth, block), lambda i, mine: (0, i)), wide_spec, wide_spec, wide_spec],
+        ),
         out_shape=[jax.ShapeDtypeStruct((tokens, depth), jnp.bfloat16), jax.ShapeDtypeStruct((depth, tokens), jnp.bfloat16)] + [jax.ShapeDtypeStruct((tokens, 128), t) for t in (jnp.float32, jnp.float32, jnp.int32)],
         compiler_params=pltpu.CompilerParams(vmem_limit_bytes=VMEM_LIMIT, dimension_semantics=('arbitrary',)),
         cost_estimate=pl.CostEstimate(flops=8 * tokens * depth, bytes_accessed=8 * tokens * depth, transcendentals=0),
         name='prep_pass',
-    )(x_all, norm_gain[None], lse[:, None], scale[:, None], lab[:, None])
-
-
-def dw_kernel(n, halves, n_recv, lanes, has_prev, cols_ref, rcols_ref, w_ref, xn_hbm, xt_hbm, lse_hbm, scale_hbm, lab_hbm, *rest):
+    )(mine, x_all, norm_gain[None], *stats)
+
+
+def dw_kernel(n, entry, halves, n_recv, lanes, has_prev, bases_ref, w_ref, xn_hbm, xt_hbm, lse_hbm, scale_hbm, lab_hbm, *rest):
     recvs = rest[:n_recv]
     rest = rest[n_recv + (1 if has_prev else 0):]
     out_ref = rest[0]
@@ -153,14 +161,15 @@
         part = pl.ds(pl.multiple_of(t * row, row), row)
         return pltpu.make_async_copy(xt_hbm.at[part, :], xt.at[part, :], in_sem.at[N_CHUNK + t])
 
-    def stat_copies():
-        return [pltpu.make_async_copy(src, dst, st_sem.at[k]) for k, (src, dst) in enumerate(((lse_hbm, lse_v), (scale_hbm, scale_v), (lab_hbm, lab_v)))]
+    def stat_copies(t):
+        part = pl.ds(pl.multiple_of(t * tok, tok), tok)
+        return [pltpu.make_async_copy(src.at[part, :], dst.at[part, :], st_sem.at[k, t]) for k, (src, dst) in enumerate(((lse_hbm, lse_v), (scale_hbm, scale_v), (lab_hbm, lab_v)))]
 
     def tile(ref, r, block):
         return ref.at[pl.ds(pl.multiple_of(r * row, row), row), pl.ds(pl.multiple_of(block * BN, BN), BN)]
 
     def out_copy(step, t, slot):
-        return pltpu.make_async_copy(o_buf.at[slot], tile(out_ref, t, cols_ref[step]), out_sem.at[slot])
+        return pltpu.make_async_copy(o_buf.at[slot], tile(out_ref, t, bases_ref[entry] + step), out_sem.at[slot])
 
     def send_copy(k, r, block, slot):
         return pltpu.make_async_copy(o_buf.at[slot], tile(sends[k], r, block), send_sem.at[slot])
@@ -181,12 +190,12 @@
         for lane, entries in enumerate(lanes):
             total = sum(entry[4] for entry in entries)
             at = 0
-            for k, first_col, first_row, u0, count, per_block in entries:
+            for k, where, first_row, u0, count, per_block in entries:
                 @pl.when((v >= at + 1) & (v < at + 1 + count))
-                def _(at=at, first_col=first_col, first_row=first_row, u0=u0, per_block=per_block):
+                def _(at=at, where=where, first_row=first_row, u0=u0, per_block=per_block):
                     u = v - 1 - at + u0
                     rin_copy(lane, recvs[0], 0, 0, other).wait()
-                    rout_copy(lane, first_row + lax.rem(u, per_block), rcols_ref[first_col + u // per_block], other).start()
+                    rout_copy(lane, first_row + lax.rem(u, per_block), bases_ref[where] + u // per_block, other).start()
 
                 at += count
 
@@ -195,7 +204,7 @@
                 rout_copy(lane, 0, 0, slot).wait()
 
             at = 0
-            for k, first_col, first_row, u0, count, per_block in entries:
+            for k, where, first_row, u0, count, per_block in entries:
                 @pl.when((v >= at) & (v < at + count))
                 def _(at=at, k=k, u0=u0, per_block=per_block):
                     u = v - at + u0
@@ -208,7 +217,7 @@
         z = jnp.dot(xn[part, :], w_ref[...], preferred_element_type=jnp.float32)
         lse, scale, lab = lse_v[part, :], scale_v[part, :], lab_v[part, :]
         lane_id = lax.broadcasted_iota(jnp.int32, (tok, 128), 1)
-        first = cols_ref[jnp.minimum(i, n - 1)] * BN
+        first = (bases_ref[entry] + jnp.minimum(i, n - 1)) * BN
         for k in range(BN // 128):
             prob = jnp.exp(z[:, k * 128:(k + 1) * 128] - lse)
             hit = lab == lane_id + (first + k * 128)
@@ -245,10 +254,14 @@
                     xt_copy(t).wait()
             else:
                 xn_copy(t).wait()
+                for copy in stat_copies(t):
+                    copy.wait()
 
                 @pl.when(t + 2 < N_CHUNK)
                 def _():
                     xn_copy(t + 2).start()
+                    for copy in stat_copies(t + 2):
+                        copy.start()
 
                 xt_copy(t).start()
             if do_dz:
@@ -262,12 +275,10 @@
 
     @pl.when(i == 0)
     def _():
-        xn_copy(0).start()
-        for copy in stat_copies():
-            copy.start()
-        xn_copy(1).start()
-        for copy in stat_copies():
-            copy.wait()
+        for t in range(2):
+            xn_copy(t).start()
+            for copy in stat_copies(t):
+                copy.start()
         loop(True, False)
 
     @pl.when((i > 0) & (i < n))
@@ -283,8 +294,8 @@
 
 def plan_lanes(recvs, row, n):
     room = (n + 1) * N_CHUNK - 2
-    lanes, left, first_col = [], 0, 0
-    for k, (array, first_row) in enumerate(recvs):
+    lanes, left = [], 0
+    for k, (array, first_row, where) in enumerate(recvs):
         per_block = array.shape[0] // row
         total = per_block * (array.shape[1] // BN)
         done = 0
@@ -293,20 +304,18 @@
                 lanes.append([])
                 left = room
             take = min(left, total - done)
-            lanes[-1].append((k, first_col, first_row, done, take, per_block))
+            lanes[-1].append((k, where, first_row, done, take, per_block))
             done += take
             left -= take
-        first_col += array.shape[1] // BN
     return tuple(tuple(lane) for lane in lanes)
 
 
-def dw_pass(cols, halves, recvs, rcols, prev, w_head, xn, xt, lse, scale, lab):
-    n = cols.shape[0]
+def dw_pass(n, entry, bases, halves, recvs, prev, w_head, xn, xt, lse, scale, lab):
     depth, vocab = w_head.shape
     tokens = xn.shape[0]
     row = depth // N_CHUNK
     hbm = pl.BlockSpec(memory_space=pl.ANY)
-    operands = [w_head, xn, xt, lse, scale, lab, *[r for r, _ in recvs]]
+    operands = [w_head, xn, xt, lse, scale, lab, *[r for r, _, _ in recvs]]
     if prev is not None:
         operands.append(prev)
     lanes = plan_lanes(recvs, row, n)
@@ -314,9 +323,9 @@
     send_rows = [depth // 2] * 2 if halves else [depth]
     out_shape = [jax.ShapeDtypeStruct((depth, vocab), jnp.float32)] + [jax.ShapeDtypeStruct((r, n * BN), jnp.float32) for r in send_rows]
     grid_spec = pltpu.PrefetchScalarGridSpec(
-        num_scalar_prefetch=2,
+        num_scalar_prefetch=1,
         grid=(n + 1,),
-        in_specs=[pl.BlockSpec((depth, BN), lambda i, cols, rcols: (0, cols[jnp.minimum(i, n - 1)]))] + [hbm] * (len(operands) - 1),
+        in_specs=[pl.BlockSpec((depth, BN), lambda i, bases: (0, bases[entry] + jnp.minimum(i, n - 1)))] + [hbm] * (len(operands) - 1),
         out_specs=[hbm] * len(out_shape),
         scratch_shapes=[
             pltpu.VMEM((tokens, depth), jnp.bfloat16),
@@ -328,7 +337,7 @@
             pltpu.VMEM((2, row, BN), jnp.float32),
             pltpu.VMEM((2, n_lanes, row, BN) if lanes else (2, 1, 8, 128), jnp.float32),
             pltpu.SemaphoreType.DMA((2 * N_CHUNK,)),
-            pltpu.SemaphoreType.DMA((3,)),
+            pltpu.SemaphoreType.DMA((3, N_CHUNK)),
             pltpu.SemaphoreType.DMA((2,)),
             pltpu.SemaphoreType.DMA((2,)),
             pltpu.SemaphoreType.DMA((2, n_lanes)),
@@ -337,62 +346,72 @@
     )
     width = n * BN
     return pl.pallas_call(
-        functools.partial(dw_kernel, n, halves, len(recvs), lanes, prev is not None),
+        functools.partial(dw_kernel, n, entry, halves, len(recvs), lanes, prev is not None),
         grid_spec=grid_spec,
         out_shape=out_shape,
-        input_output_aliases={} if prev is None else {2 + len(operands) - 1: 0},
+        input_output_aliases={} if prev is None else {1 + len(operands) - 1: 0},
         compiler_params=pltpu.CompilerParams(vmem_limit_bytes=VMEM_LIMIT, dimension_semantics=('arbitrary',)),
         cost_estimate=pl.CostEstimate(flops=4 * tokens * depth * width, bytes_accessed=depth * width * 10, transcendentals=tokens * width),
-    )(cols, rcols, *operands)
-
-
-def place_kernel(n_recv, starts, at_row, at_col, *refs):
-    recvs, out_ref = refs[:n_recv], refs[n_recv + 1]
-    i = pl.program_id(0)
-    for k, ref in enumerate(recvs):
-        @pl.when((i >= starts[k]) & (i < starts[k + 1]))
-        def _(ref=ref):
-            out_ref[...] = ref[...]
-
-
-def place_pass(recvs, rcols, prev):
+    )(bases, *operands)
+
+
+def place_kernel(tiles, n_recv, bases_ref, *rest):
+    recvs = rest[:n_recv]
+    out_ref, buf, in_sem, out_sem = rest[n_recv + 1:]
+    slots = buf.shape[0]
+
+    def tile(ref, r, block):
+        half = buf.shape[1]
+        return ref.at[pl.ds(r * half, half), pl.ds(pl.multiple_of(block * BN, BN), BN)]
+
+    def load(u):
+        k, r, block, _, _ = tiles[u]
+        return pltpu.make_async_copy(tile(recvs[k], r, block), buf.at[u % slots], in_sem.at[u % slots])
+
+    def store(u):
+        _, _, block, to_row, where = tiles[u]
+        return pltpu.make_async_copy(buf.at[u % slots], tile(out_ref, to_row, bases_ref[where] + block), out_sem.at[u % slots])
+
+    ahead = slots // 2
+    n = len(tiles)
+    for u in range(min(ahead, n)):
+        load(u).start()
+    for u in range(n):
+        load(u).wait()
+        store(u).start()
+        if u + ahead < n:
+            if u + ahead >= slots:
+                store(u + ahead - slots).wait()
+            load(u + ahead).start()
+    for u in range(max(n - slots, 0), n):
+        store(u).wait()
+
+
+def place_pass(recvs, bases, prev):
     depth = prev.shape[0]
     half = depth // 2
-    steps, sizes, first_col = [], [], 0
-    for array, first_row in recvs:
-        per_block = array.shape[0] // half
+    tiles = []
+    for k, (array, first_row, where) in enumerate(recvs):
         for block in range(array.shape[1] // BN):
-            for r in range(per_block):
-                steps.append((first_row // (N_CHUNK // 2) + r, first_col + block))
-        first_col += array.shape[1] // BN
-        sizes.append((per_block, per_block * (array.shape[1] // BN)))
-    starts = [0] + [int(v) for v in np.cumsum([size for _, size in sizes])]
-    at_row = jnp.asarray([r for r, _ in steps], jnp.int32)
-    at_col = rcols[np.asarray([c for _, c in steps])]
-
-    def recv_spec(k):
-        per_block, size = sizes[k]
-
-        def at(i, at_row, at_col):
-            u = jnp.clip(i - starts[k], 0, size - 1)
-            return lax.rem(u, per_block), lax.div(u, per_block)
-
-        return pl.BlockSpec((half, BN), at)
-
+            for r in range(array.shape[0] // half):
+                tiles.append((k, r, block, first_row // (N_CHUNK // 2) + r, where))
+    hbm = pl.BlockSpec(memory_space=pl.ANY)
+    slots = 12
     return pl.pallas_call(
-        functools.partial(place_kernel, len(recvs), tuple(starts)),
+        functools.partial(place_kernel, tuple(tiles), len(recvs)),
         grid_spec=pltpu.PrefetchScalarGridSpec(
-            num_scalar_prefetch=2,
-            grid=(starts[-1],),
-            in_specs=[recv_spec(k) for k in range(len(recvs))] + [pl.BlockSpec(memory_space=pl.ANY)],
-            out_specs=pl.BlockSpec((half, BN), lambda i, at_row, at_col: (at_row[i], at_col[i])),
+            num_scalar_prefetch=1,
+            grid=(1,),
+            in_specs=[hbm] * (len(recvs) + 1),
+            out_specs=hbm,
+            scratch_shapes=[pltpu.VMEM((slots, half, BN), jnp.float32), pltpu.SemaphoreType.DMA((slots,)), pltpu.SemaphoreType.DMA((slots,))],
         ),
         out_shape=jax.ShapeDtypeStruct(prev.shape, prev.dtype),
-        input_output_aliases={2 + len(recvs): 0},
+        input_output_aliases={1 + len(recvs): 0},
         compiler_params=pltpu.CompilerParams(vmem_limit_bytes=VMEM_LIMIT, dimension_semantics=('arbitrary',)),
-        cost_estimate=pl.CostEstimate(flops=half * BN * starts[-1], bytes_accessed=8 * half * BN * starts[-1], transcendentals=0),
+        cost_estimate=pl.CostEstimate(flops=40 * half * BN * len(tiles), bytes_accessed=8 * half * BN * len(tiles), transcendentals=0),
         name='place_pass',
-    )(at_row, at_col, *[r for r, _ in recvs], prev)
+    )(bases, *[r for r, _, _ in recvs], prev)
 
 
 def solution(mesh):
@@ -423,40 +442,45 @@
         x_norm = (x_hat * norm_gain).astype(jnp.bfloat16)
         x_all = lax.all_gather(x_hat, ('cp', 'dp'), tiled=True)
 
-        next_first = lax.ppermute(tokens[:, 0], 'cp', from_next_pairs)
-        prev_second = lax.ppermute(tokens[:, seg_len], 'cp', from_prev_pairs)
-        first_end = jnp.where(cp_rank == cp_size - 1, tokens[:, seg_len], next_first)
-        labels = jnp.concatenate([tokens[:, 1:seg_len], first_end[:, None], tokens[:, seg_len + 1:], prev_second[:, None]], axis=1)
+        heads = lax.optimization_barrier((tokens[:, :1], tokens[:, seg_len:seg_len + 1]))
+        next_first = swap(heads[0], 'cp', from_next_pairs)
+        prev_second = swap(heads[1], 'cp', from_prev_pairs)
+        first_end = jnp.where(cp_rank == cp_size - 1, heads[1], next_first)
+        shifted = jnp.concatenate([tokens[:, 1:], tokens[:, :1]], axis=1)
+        column = jnp.arange(local_len)[None]
+        labels = jnp.where(column == seg_len - 1, first_end, jnp.where(column == local_len - 1, prev_second, shifted))
         seg_pos = jnp.arange(seg_len)
         positions = jnp.concatenate([cp_rank * seg_len + seg_pos, (2 * cp_size - 1 - cp_rank) * seg_len + seg_pos])
         valid_mask = (positions[None, :] + 1 < seq_lens[:, None]).astype(jnp.float32)
 
-        z, m_lane, s_lane = logits_pass(x_norm, w_head, 1024)
+        len_sum = jnp.full((128,), jnp.sum(seq_lens - 1).astype(jnp.float32))
+        len_parts = [swap(len_sum, 'dp', [(d, d ^ k) for d in range(dp_size)]) for k in range(1, dp_size)]
+
+        z, m_lane, s_lane = logits_pass(x_norm, w_head, 2048)
+        valid_count = functools.reduce(jnp.add, len_parts, len_sum)[0]
         m_loc = jnp.max(m_lane, axis=-1)
         s_loc = jnp.sum(s_lane * jnp.exp(m_lane - m_loc[:, None]), axis=-1)
-
-        stats = jnp.stack([m_loc, s_loc, labels.reshape(rows).astype(jnp.float32), valid_mask.reshape(rows)])
-        stats = lax.all_gather(stats, ('tp', 'cp', 'dp')).reshape(tp_size, cp_size * dp_size, 4, rows)
-        glob_max = jnp.max(stats[:, :, 0], axis=0)
-        log_norm_all = glob_max + jnp.log(jnp.sum(stats[:, :, 1] * jnp.exp(stats[:, :, 0] - glob_max), axis=0))
-        valid_all = stats[0, :, 3]
-        valid_count = jnp.sum(valid_all)
-        scale_all = valid_all / valid_count
-        lab_f32 = stats[0, :, 2] - (tp_rank * vocab_local).astype(jnp.float32)
+        m_far, s_far = swap(jnp.stack([m_loc, s_loc]), 'tp', tp_swap)
+        glob_max = jnp.maximum(m_loc, m_far)
+        log_norm = glob_max + jnp.log(s_loc * jnp.exp(m_loc - glob_max) + s_far * jnp.exp(m_far - glob_max))
+        tok_scale = valid_mask.reshape(rows) / valid_count
+        local_lab = labels.reshape(rows) - tp_rank * vocab_local
+
+        stats = jnp.stack([log_norm, local_lab.astype(jnp.float32), tok_scale])
+        n_group = cp_size * dp_size
+        dx_rows = (log_norm, tok_scale, local_lab)
+        stats, dx_rows = lax.optimization_barrier((stats, dx_rows))
+        far_stats = [swap(stats, ('cp', 'dp'), [(d, d ^ k) for d in range(n_group)]) for k in range(1, n_group)]
+        stats_all = [stats, *far_stats]
+        mine = cp_rank * dp_size + dp_rank
 
         def wide(v):
             return jnp.broadcast_to(v.reshape(-1, 1), (v.size, 128))
 
-        mine = cp_rank * dp_size + dp_rank
-
-        def own(v):
-            return lax.dynamic_index_in_dim(v, mine, axis=0, keepdims=False)
-
-        log_norm = own(log_norm_all)
-        dx_part, t_lane = dx_pass(z, w_head, wide(log_norm), wide(own(scale_all)), wide(own(lab_f32).astype(jnp.int32)), 1024)
+        dx_part, t_lane = dx_pass(z, w_head, *[wide(v) for v in dx_rows], 1024)
         t_part = jnp.sum(t_lane, axis=-1)
         dx_part, x_all = lax.optimization_barrier((dx_part, x_all))
-        xn_all, xt_all, lse_w, scale_w, lab_w = prep_pass(x_all, norm_gain, log_norm_all, scale_all, lab_f32)
+        xn_all, xt_all, lse_w, scale_w, lab_w = prep_pass(mine[None].astype(jnp.int32), x_all, norm_gain, stats_all)
         dx_norm = dx_part + swap(dx_part, 'tp', tp_swap)
         target_logit = t_part + swap(t_part, 'tp', tp_swap)
         tok_loss = (log_norm - target_logit).reshape(n_seqs, local_len) * valid_mask
@@ -476,57 +500,63 @@
         assert 4 * n_shared + 2 * n_common == n_blocks
         role = (dp_rank // 2 + cp_rank) % 2
 
-        def shared_cols(k, who, part):
+        table, entries = [], {}
+
+        def add(name, const, by_role, by_core):
+            entries[name] = len(table)
+            table.append((const, by_role, by_core))
+
+        for k in range(len(shared)):
             first = sum(shared[:k])
-            return (who * 2 * n_shared + part * n_shared + first + jnp.arange(shared[k])).astype(jnp.int32)
-
-        def common_cols(k, part):
-            first = sum(common[:k])
-            return (4 * n_shared + part * n_common + first + jnp.arange(common[k])).astype(jnp.int32)
+            add(('mine', k), first, 2 * n_shared, n_shared)
+            add(('core', k), first + n_shared, 2 * n_shared, -n_shared)
+            add(('chip', k), first + 2 * n_shared, -2 * n_shared, n_shared)
+            add(('pass', k), first + 3 * n_shared, -2 * n_shared, -n_shared)
+        for k in range(len(common)):
+            first = 4 * n_shared + sum(common[:k])
+            add(('all', k), first, 0, n_common)
+            add(('core_all', k), first + n_common, 0, -n_common)
+        parts = np.asarray(table, np.int32).T
+        bases = (parts[0] + parts[1] * role + parts[2] * core).astype(jnp.int32)
 
         lower = N_CHUNK // 2
         out = None
 
-        def run(cols, halves, arrived):
-            recvs = [pair for pair, _ in arrived]
-            rcols = jnp.concatenate([c for _, c in arrived]) if arrived else jnp.zeros((1,), jnp.int32)
-            return dw_pass(cols, halves, recvs, rcols, out, w_head, xn_all, xt_all, lse_w, scale_w, lab_w)
+        def run(n, entry, halves, arrived):
+            return dw_pass(n, entries[entry], bases, halves, arrived, out, w_head, xn_all, xt_all, lse_w, scale_w, lab_w)
 
         from_core, from_chip, passed_on, from_core_common = {}, {}, {}, {}
 
         def share(k, send_x, send_y):
-            cols = shared_cols(k, role, 1 - core)
-            from_core[k] = [((swap(send_x, 'dp', core_swap), 0), cols), ((swap(send_y, 'dp', core_swap), lower), cols)]
-            cols = shared_cols(k, 1 - role, core)
-            from_chip[k] = [((swap(send_x, 'dp', x_swap), 0), cols), ((swap(send_y, 'cp', cp_swap), lower), cols)]
+            where = entries['core', k]
+            from_core[k] = [(swap(send_x, 'dp', core_swap), 0, where), (swap(send_y, 'dp', core_swap), lower, where)]
+            where = entries['chip', k]
+            from_chip[k] = [(swap(send_x, 'dp', x_swap), 0, where), (swap(send_y, 'cp', cp_swap), lower, where)]
 
         def pass_on(k):
             nonlocal out
-            cols = shared_cols(k, 1 - role, 1 - core)
-            (up, _), (low, _) = [pair for pair, _ in from_chip[k]]
-            up, low, out = lax.optimization_barrier((up, low, out))
-            from_chip[k] = [((up, 0), from_chip[k][0][1]), ((low, lower), from_chip[k][1][1])]
-            passed_on[k] = [((swap(up, 'dp', core_swap), 0), cols), ((swap(low, 'dp', core_swap), lower), cols)]
+            where = entries['chip', k]
+            up, low, out = lax.optimization_barrier((from_chip[k][0][0], from_chip[k][1][0], out))
+            from_chip[k] = [(up, 0, where), (low, lower, where)]
+            where = entries['pass', k]
+            passed_on[k] = [(swap(up, 'dp', core_swap), 0, where), (swap(low, 'dp', core_swap), lower, where)]
 
         def share_common(k, send):
-            from_core_common[k] = [((swap(send, 'dp', core_swap), 0), common_cols(k, 1 - core))]
-
-        out, *sent = run(shared_cols(0, role, core), True, [])
-        share(0, *sent)
-        out, *sent = run(shared_cols(1, role, core), True, [])
-        share(1, *sent)
-        out, *sent = run(common_cols(0, core), False, from_core[0])
-        share_common(0, *sent)
+            from_core_common[k] = [(swap(send, 'dp', core_swap), 0, entries['core_all', k])]
+
+        for k in range(2):
+            out, *sent = run(shared[k], ('mine', k), True, [])
+            share(k, *sent)
+        out, send = run(common[0], ('all', 0), False, from_core[0])
+        share_common(0, send)
         pass_on(0)
-        out, *sent = run(common_cols(1, core), False, from_core[1] + from_chip[0])
-        share_common(1, *sent)
-        out, *sent = run(common_cols(2, core), False, passed_on[0] + from_core_common[0])
-        share_common(2, *sent)
+        out, send = run(common[1], ('all', 1), False, from_core[1] + from_chip[0])
+        share_common(1, send)
         pass_on(1)
-        out, *sent = run(common_cols(3, core), False, from_chip[1] + from_core_common[1])
-        share_common(3, *sent)
-        last = passed_on[1] + from_core_common[2] + from_core_common[3]
-        d_head = place_pass([pair for pair, _ in last], jnp.concatenate([c for _, c in last]), out)
+        out, send = run(common[2], ('all', 2), False, passed_on[0] + from_core_common[0] + from_chip[1])
+        share_common(2, send)
+        out = place_pass(passed_on[1] + from_core_common[1], bases, out)
+        d_head = place_pass(from_core_common[2], bases, out)
         return tok_loss, loss_mean, d_hidden.reshape(hidden.shape), d_gain, d_head
 
     return jax.shard_map(local_fn, mesh=mesh, in_specs=(P('dp', 'cp', None), P('dp', 'cp'), P('dp'), P(None), P(None, 'tp')), out_specs=(P('dp', 'cp'), P(), P('dp', 'cp', None), P(None), P(None, 'tp')), check_vma=False)

time: 947 us -> 990 us (1.045)
  waiting for transfers between devices: 205 us -> 270 us
  blocking collectives: 16.6 us -> 0 us
  starting transfers between devices: 15.6 us -> 31.2 us
  Pallas kernels: 640 us -> 627 us
    ppermute x21 -> x33, waiting for transfers between devices: 205 us -> 270 us  [swap(): return lax.ppermute(v, axis, pairs)]
    ppermute x21 -> x33, starting transfers between devices: 9.19 us -> 31.2 us  [swap(): return lax.ppermute(v, axis, pairs)]
    all_gather x1 -> x0, blocking collectives: 16.6 us -> none  [local_fn(): lax.all_gather(stats, ('tp', 'cp', 'dp'))]
  transfers between devices with their start and end apart: 24 -> 34, of which waited for: 8 -> 8; matrix products, arithmetic and copies ran while one was open for 4% -> 3% of each run, Pallas kernels for 49% -> 44%
where the time goes in v2:
time: 990 us; the launch traced here: 982 us
  Pallas kernels  627 us (63%)
  waiting for transfers between devices  270 us (27%)
  starting transfers between devices  31.2 us (3%)
  other arithmetic  28.1 us (3%)
  between operations  17.2 us (2%)
    pallas_call x5, Pallas kernels, dw_pass(): pl.pallas_call(functools.partial(dw_kernel, n, entry, halves, len(recvs),...  426 us
    ppermute x33, waiting for transfers between devices, swap(): return lax.ppermute(v, axis, pairs)  270 us
    pallas_call x1, Pallas kernels, dx_pass(): pl.pallas_call(functools.partial(dx_kernel, n_blocks), grid=(n_blocks + 1...  76.9 us
    pallas_call x1, Pallas kernels, logits_pass(): pl.pallas_call(logits_kernel, grid=(vocab // block,), in_specs=[pl.BlockS...  66 us
    pallas_call x2, Pallas kernels, place_pass(): pl.pallas_call(functools.partial(place_kernel, tuple(tiles), len(recvs)),...  33.6 us
    ppermute x33, starting transfers between devices, swap(): return lax.ppermute(v, axis, pairs)  31.2 us
    pallas_call x1, Pallas kernels, prep_pass(): pl.pallas_call(prep_kernel, grid_spec=pltpu.PrefetchScalarGridSpec(num_sc...  25 us
  transfers between devices with their start and end apart: 34, of which 8 were waited for; matrix products, arithmetic and copies ran while one was open for 3% of the time, Pallas kernels for 44%

profile of v2, /device:TPU:1, one launch (start us, length us, event | category | flops | bytes accessed | tf_op | source)
XLA Modules:
  0.0 982.0 jit_solution(13519336441318091720)
XLA Ops:
  7.2 2.1 multiply_reduce_fusion.2
  9.4 4.9 bitcast_multiply_fusion
  16.7 2.7 collective-permute-start.4
  19.4 66.0 %logits_pass.1 = (f32[512,24576]{1,0:T(8,128)}, f32[512,128]{1,0:T(8,128)}, f32[512,128]{1,0:T(8,128)}) custom-call(bf16[512,2048]{1,0:T(8,128)(2,1)} %get-tuple-element.84.x_ref, bf16[2048,24576]{1,0:T(8,128)(2,1)} %w_ref.13), custom_call_target="tpu_custom_call" | custom-call | flops 51539607552 | bytes 150994944 | tf_op jit(solution)/shard_map/logits_pass/pallas_call | solution.py:43
  86.6 1.3 multiply_reduce_fusion.3
  87.9 1.7 collective-permute-start
  90.5 3.1 collective-permute-start.2
  95.2 1.6 collective-permute-start.1
  97.0 3.4 collective-permute-done.1
  103.4 1.7 collective-permute-start.11
  106.2 1.3 add_add_fusion.1.bases_ref
  108.0 1.8 collective-permute-start.15
  110.5 1.9 collective-permute-start.17
  115.0 76.9 %dx_pass.1 = (f32[512,2048]{1,0:T(8,128)}, f32[512,128]{1,0:T(8,128)}) custom-call(f32[512,24576]{1,0:T(8,128)} %get-tuple-element.43.z_ref, bf16[2048,24576]{1,0:T(8,128)(2,1)} %w_ref.13, f32[512,128]{1,0:T(8,128)} %broadcast_in_dim.70.lse_ref, f32[512,128]{1,0:T(8,128)} %broadcast_in_dim.71.scale_ref, s32[512,128]{1,0:T(8,128)} %broadcast_in_dim.72.lab_ref), custom_call_target="tpu_custom_call" | custom-call | flops 51539607552 | bytes 150994944 | tf_op jit(solution)/shard_map/dx_pass/pallas_call | solution.py:91
  191.9 25.0 %prep_pass.1 = (bf16[4096,2048]{1,0:T(8,128)(2,1)}, bf16[2048,4096]{1,0:T(8,128)(2,1)}, f32[4096,128]{1,0:T(8,128)}, f32[4096,128]{1,0:T(8,128)}, s32[4096,128]{1,0:T(8,128)}) custom-call(s32[1]{0:T(128)} %bitcast.8.mine_ref, f32[4096,2048]{1,0:T(8,128)} %all-gather.2.cloned.1.call-done.x_ref, f32[1,2048]{1,0:T(1,128)} %bitcast.21, ...), custom_call_target="tpu_custom_call" | custom-call | flops 67108864 | bytes 67108864 | tf_op jit(solution)/shard_map/prep_pass/pallas_call | solution.py:128
  216.9 48.0 %shard_map.119 = (f32[2048,24576]{1,0:T(8,128)}, f32[1024,1024]{1,0:T(8,128)}, f32[1024,1024]{1,0:T(8,128)}) custom-call(s32[14]{0:T(128)} %add_add_fusion.1.bases_ref, bf16[2048,24576]{1,0:T(8,128)(2,1)} %w_ref.13, bf16[4096,2048]{1,0:T(8,128)(2,1)} %get-tuple-element.54.xn_hbm, bf16[2048,4096]{1,0:T(8,128)(2,1)} %get-tuple-element.55.xt_hbm, ...), custom_call_target="tpu_custom_call" | custom-call | flops 34359738368 | bytes 20971520 | tf_op jit(solution)/shard_map/pallas_call | solution.py:348
  265.4 90.9 %shard_map.120 = (f32[2048,24576]{1,0:T(8,128)}, f32[1024,2048]{1,0:T(8,128)}, f32[1024,2048]{1,0:T(8,128)}) custom-call(s32[14]{0:T(128)} %add_add_fusion.1.bases_ref, bf16[2048,24576]{1,0:T(8,128)(2,1)} %w_ref.13, bf16[4096,2048]{1,0:T(8,128)(2,1)} %get-tuple-element.54.xn_hbm, ...), custom_call_target="tpu_custom_call", output_to_operand_aliasing={{0}: (7, {})} | custom-call | flops 68719476736 | bytes 41943040 | tf_op jit(solution)/shard_map/pallas_call | solution.py:348
  356.4 113.5 %shard_map.121 = (f32[2048,24576]{1,0:T(8,128)}, f32[2048,2560]{1,0:T(8,128)}) custom-call(s32[14]{0:T(128)} %add_add_fusion.1.bases_ref, bf16[2048,24576]{1,0:T(8,128)(2,1)} %w_ref.13, bf16[4096,2048]{1,0:T(8,128)(2,1)} %get-tuple-element.54.xn_hbm, bf16[2048,4096]{1,0:T(8,128)(2,1)} %get-tuple-element.55.xt_hbm, ...), custom_call_target="tpu_custom_call", output_to_operand_aliasing={{0}: (9, {})} | custom-call | flops 85899345920 | bytes 52428800 | tf_op jit(solution)/shard_map/pallas_call | solution.py:348
  471.7 90.8 %collective-permute-done.18.rest_2_ = f32[1024,1024]{1,0:T(8,128)} collective-permute-done((f32[1024,1024]{1,0:T(8,128)}, f32[1024,1024]{1,0:T(8,128)}, u32[]{:S(2)}, u32[]{:S(2)}) %collective-permute-start.18) | collective-permute-done | bytes 4194336 | tf_op jit(solution)/shard_map/ppermute | solution.py:437
  564.1 1.5 collective-permute-start.22
  565.6 94.7 %shard_map.122 = (f32[2048,24576]{1,0:T(8,128)}, f32[2048,2048]{1,0:T(8,128)}) custom-call(s32[14]{0:T(128)} %add_add_fusion.1.bases_ref, bf16[2048,24576]{1,0:T(8,128)(2,1)} %w_ref.13, bf16[4096,2048]{1,0:T(8,128)(2,1)} %get-tuple-element.54.xn_hbm, bf16[2048,4096]{1,0:T(8,128)(2,1)} %get-tuple-element.55.xt_hbm, ...), custom_call_target="tpu_custom_call", output_to_operand_aliasing={{0}: (11, {})} | custom-call | flops 68719476736 | bytes 41943040 | tf_op jit(solution)/shard_map/pallas_call | solution.py:348
  660.4 83.1 %collective-permute-done.25.rest_3_ = f32[1024,2048]{1,0:T(8,128)} collective-permute-done((f32[1024,2048]{1,0:T(8,128)}, f32[1024,2048]{1,0:T(8,128)}, u32[]{:S(2)}, u32[]{:S(2)}) %collective-permute-start.25) | collective-permute-done | bytes 8388640 | tf_op jit(solution)/shard_map/ppermute | solution.py:437
  744.4 2.5 collective-permute-start.32
  746.8 78.8 %shard_map.123 = (f32[2048,24576]{1,0:T(8,128)}, f32[2048,1536]{1,0:T(8,128)}) custom-call(s32[14]{0:T(128)} %add_add_fusion.1.bases_ref, bf16[2048,24576]{1,0:T(8,128)(2,1)} %w_ref.13, bf16[4096,2048]{1,0:T(8,128)(2,1)} %get-tuple-element.54.xn_hbm, bf16[2048,4096]{1,0:T(8,128)(2,1)} %get-tuple-element.55.xt_hbm, ...), custom_call_target="tpu_custom_call", output_to_operand_aliasing={{0}: (12, {})} | custom-call | flops 51539607552 | bytes 31457280 | tf_op jit(solution)/shard_map/pallas_call | solution.py:348
  831.0 1.3 select_reduce_fusion.1
  832.4 88.2 %collective-permute-done.7 = f32[512,2048]{1,0:T(8,128)} collective-permute-done((f32[512,2048]{1,0:T(8,128)}, f32[512,2048]{1,0:T(8,128)}, u32[]{:S(2)}, u32[]{:S(2)}) %collective-permute-start.7) | collective-permute-done | bytes 4194336 | tf_op jit(solution)/shard_map/ppermute | solution.py:437
  920.6 5.3 multiply_reduce_fusion
  926.6 2.5 collective-permute-start.8
  931.0 2.2 collective-permute-done.9
  933.7 4.6 multiply_convert_fusion
  940.1 23.9 %place_pass.2.rest_1_ = f32[2048,24576]{1,0:T(8,128)} custom-call(s32[14]{0:T(128)} %add_add_fusion.1.bases_ref, f32[1024,2048]{1,0:T(8,128)} %collective-permute-done.30.rest_0_, f32[1024,2048]{1,0:T(8,128)} %collective-permute-done.31.rest_1_, f32[2048,2048]{1,0:T(8,128)} %collective-permute-done.32.rest_2_, ...), custom_call_target="tpu_custom_call", output_to_operand_aliasing={{}: (4, {})} | custom-call | flops 335544320 | bytes 67108864 | tf_op jit(solution)/shard_map/place_pass/pallas_call | solution.py:400
  964.0 9.7 place_pass.3
  (122 shorter events, 28.0 us)
Async XLA Ops:
  7.2 184.7 %all-gather.2.cloned.1.call-start = ((), (), s32[]{:S(2)}) async-start(), calls=%async_computation | async-start | bytes 37748736 | tf_op jit(solution)/shard_map/all_gather | solution.py:443
  16.7 84.0 %collective-permute-start.3 = (f32[128]{0:T(128)}, f32[128]{0:T(128)}, u32[]{:S(2)}, u32[]{:S(2)}) collective-permute-start(f32[128]{0:T(128)} %broadcast_in_dim.69), channel_id=1, source_target_pairs={{0,1},{1,0},{2,3},{3,2},{4,5},{5,4},{6,7},{7,6},{8,9},{9,8},{10,11... | collective-permute-start | bytes 1544 | tf_op jit(solution)/shard_map/ppermute | solution.py:437
  16.7 84.0 %collective-permute-start.4 = (f32[128]{0:T(128)}, f32[128]{0:T(128)}, u32[]{:S(2)}, u32[]{:S(2)}) collective-permute-start(f32[128]{0:T(128)} %broadcast_in_dim.69), channel_id=1, source_target_pairs={{0,2},{1,3},{2,0},{3,1},{4,6},{5,7},{6,4},{7,5},{8,10},{9,11},{10,... | collective-permute-start | bytes 1544 | tf_op jit(solution)/shard_map/ppermute | solution.py:437
  19.4 81.3 %collective-permute-start.5 = (f32[128]{0:T(128)}, f32[128]{0:T(128)}, u32[]{:S(2)}, u32[]{:S(2)}) collective-permute-start(f32[128]{0:T(128)} %broadcast_in_dim.69), channel_id=1, source_target_pairs={{0,3},{1,2},{2,1},{3,0},{4,7},{5,6},{6,5},{7,4},{8,11},{9,10},{10,... | collective-permute-start | bytes 1544 | tf_op jit(solution)/shard_map/ppermute | solution.py:437
  87.9 14.8 %collective-permute-start = (f32[2,512]{1,0:T(2,128)S(1)}, f32[2,512]{1,0:T(2,128)S(1)}, u32[]{:S(2)}, u32[]{:S(2)}) collective-permute-start(f32[2,512]{1,0:T(2,128)S(1)} %pad_maximum_fusion.1), channel_id=1, source_target_pairs={{0,8},{8,0},{1,9},{9,1},{2,10},{10,2},{3,11},{11,3},{4,12},{12,4},... | collective-permute-start | bytes 12296 | tf_op jit(solution)/shard_map/ppermute | solution.py:437
  90.5 4.8 collective-permute-start.2
  95.2 5.1 collective-permute-start.1
  103.4 6.5 collective-permute-start.11
  105.1 5.4 collective-permute-start.12
  107.5 84.4 %collective-permute-start.13 = (f32[3,512]{1,0:T(4,128)}, f32[3,512]{1,0:T(4,128)}, u32[]{:S(2)}, u32[]{:S(2)}) collective-permute-start(f32[3,512]{1,0:T(4,128)} %pad_maximum_fusion.refs_0_), channel_id=1, source_target_pairs={{0,3},{1,2},{2,1},{3,0},{4,7},{5,6},{6,5},{7,4},{8,11},{9,10},{10,... | collective-permute-start | bytes 18440 | tf_op jit(solution)/shard_map/ppermute | solution.py:437
  108.0 83.9 %collective-permute-start.14 = (f32[3,512]{1,0:T(4,128)}, f32[3,512]{1,0:T(4,128)}, u32[]{:S(2)}, u32[]{:S(2)}) collective-permute-start(f32[3,512]{1,0:T(4,128)} %pad_maximum_fusion.refs_0_), channel_id=1, source_target_pairs={{0,4},{1,5},{2,6},{3,7},{4,0},{5,1},{6,2},{7,3},{8,12},{9,13},{10,... | collective-permute-start | bytes 18440 | tf_op jit(solution)/shard_map/ppermute | solution.py:437
  108.0 83.9 %collective-permute-start.15 = (f32[3,512]{1,0:T(4,128)}, f32[3,512]{1,0:T(4,128)}, u32[]{:S(2)}, u32[]{:S(2)}) collective-permute-start(f32[3,512]{1,0:T(4,128)} %pad_maximum_fusion.refs_0_), channel_id=1, source_target_pairs={{0,5},{1,4},{2,7},{3,6},{4,1},{5,0},{6,3},{7,2},{8,13},{9,12},{10,... | collective-permute-start | bytes 18440 | tf_op jit(solution)/shard_map/ppermute | solution.py:437
  109.8 82.1 %collective-permute-start.16 = (f32[3,512]{1,0:T(4,128)}, f32[3,512]{1,0:T(4,128)}, u32[]{:S(2)}, u32[]{:S(2)}) collective-permute-start(f32[3,512]{1,0:T(4,128)} %pad_maximum_fusion.refs_0_), channel_id=1, source_target_pairs={{0,6},{1,7},{2,4},{3,5},{4,2},{5,3},{6,0},{7,1},{8,14},{9,15},{10,... | collective-permute-start | bytes 18440 | tf_op jit(solution)/shard_map/ppermute | solution.py:437
  110.5 81.4 %collective-permute-start.17 = (f32[3,512]{1,0:T(4,128)}, f32[3,512]{1,0:T(4,128)}, u32[]{:S(2)}, u32[]{:S(2)}) collective-permute-start(f32[3,512]{1,0:T(4,128)} %pad_maximum_fusion.refs_0_), channel_id=1, source_target_pairs={{0,7},{1,6},{2,5},{3,4},{4,3},{5,2},{6,1},{7,0},{8,15},{9,14},{10,... | collective-permute-start | bytes 18440 | tf_op jit(solution)/shard_map/ppermute | solution.py:437
  264.9 91.5 %collective-permute-start.20 = (f32[1024,1024]{1,0:T(8,128)}, f32[1024,1024]{1,0:T(8,128)}, u32[]{:S(2)}, u32[]{:S(2)}) collective-permute-start(f32[1024,1024]{1,0:T(8,128)} %get-tuple-element.59), channel_id=1, source_target_pairs={{0,1},{1,0},{2,3},{3,2},{4,5},{5,4},{6,7},{7,6},{8,9},{9,8},{10,11... | collective-permute-start | bytes 12582920 | tf_op jit(solution)/shard_map/ppermute | solution.py:437
  265.0 91.4 %collective-permute-start.21 = (f32[1024,1024]{1,0:T(8,128)}, f32[1024,1024]{1,0:T(8,128)}, u32[]{:S(2)}, u32[]{:S(2)}) collective-permute-start(f32[1024,1024]{1,0:T(8,128)} %get-tuple-element.60), channel_id=1, source_target_pairs={{0,1},{1,0},{2,3},{3,2},{4,5},{5,4},{6,7},{7,6},{8,9},{9,8},{10,11... | collective-permute-start | bytes 12582920 | tf_op jit(solution)/shard_map/ppermute | solution.py:437
  469.9 277.0 %collective-permute-start.24 = (f32[2048,2560]{1,0:T(8,128)}, f32[2048,2560]{1,0:T(8,128)}, u32[]{:S(2)}, u32[]{:S(2)}) collective-permute-start(f32[2048,2560]{1,0:T(8,128)} %get-tuple-element.66), channel_id=1, source_target_pairs={{0,1},{1,0},{2,3},{3,2},{4,5},{5,4},{6,7},{7,6},{8,9},{9,8},{10,11... | collective-permute-start | bytes 62914568 | tf_op jit(solution)/shard_map/ppermute | solution.py:437
  470.0 94.1 %collective-permute-start.27 = (f32[1024,2048]{1,0:T(8,128)}, f32[1024,2048]{1,0:T(8,128)}, u32[]{:S(2)}, u32[]{:S(2)}) collective-permute-start(f32[1024,2048]{1,0:T(8,128)} %get-tuple-element.67), channel_id=1, source_target_pairs={{0,1},{1,0},{2,3},{3,2},{4,5},{5,4},{6,7},{7,6},{8,9},{9,8},{10,11... | collective-permute-start | bytes 25165832 | tf_op jit(solution)/shard_map/ppermute | solution.py:437
  470.4 95.2 %collective-permute-start.28 = (f32[1024,2048]{1,0:T(8,128)}, f32[1024,2048]{1,0:T(8,128)}, u32[]{:S(2)}, u32[]{:S(2)}) collective-permute-start(f32[1024,2048]{1,0:T(8,128)} %get-tuple-element.68), channel_id=1, source_target_pairs={{0,1},{1,0},{2,3},{3,2},{4,5},{5,4},{6,7},{7,6},{8,9},{9,8},{10,11... | collective-permute-start | bytes 25165832 | tf_op jit(solution)/shard_map/ppermute | solution.py:437
  470.5 92.0 %collective-permute-start.18 = (f32[1024,1024]{1,0:T(8,128)}, f32[1024,1024]{1,0:T(8,128)}, u32[]{:S(2)}, u32[]{:S(2)}) collective-permute-start(f32[1024,1024]{1,0:T(8,128)} %get-tuple-element.59), channel_id=1, source_target_pairs={{0,2},{1,3},{2,0},{3,1},{4,6},{5,7},{6,4},{7,5},{8,10},{9,11},{10,... | collective-permute-start | bytes 12582920 | tf_op jit(solution)/shard_map/ppermute | solution.py:437
  471.6 92.0 %collective-permute-start.19 = (f32[1024,1024]{1,0:T(8,128)}, f32[1024,1024]{1,0:T(8,128)}, u32[]{:S(2)}, u32[]{:S(2)}) collective-permute-start(f32[1024,1024]{1,0:T(8,128)} %get-tuple-element.60), channel_id=1, source_target_pairs={{0,4},{4,0},{1,5},{5,1},{2,6},{6,2},{3,7},{7,3},{8,12},{12,8},{9,1... | collective-permute-start | bytes 12582920 | tf_op jit(solution)/shard_map/ppermute | solution.py:437
  562.5 181.0 %collective-permute-start.25 = (f32[1024,2048]{1,0:T(8,128)}, f32[1024,2048]{1,0:T(8,128)}, u32[]{:S(2)}, u32[]{:S(2)}) collective-permute-start(f32[1024,2048]{1,0:T(8,128)} %get-tuple-element.67), channel_id=1, source_target_pairs={{0,2},{1,3},{2,0},{3,1},{4,6},{5,7},{6,4},{7,5},{8,10},{9,11},{10,... | collective-permute-start | bytes 25165832 | tf_op jit(solution)/shard_map/ppermute | solution.py:437
  563.6 180.7 %collective-permute-start.26 = (f32[1024,2048]{1,0:T(8,128)}, f32[1024,2048]{1,0:T(8,128)}, u32[]{:S(2)}, u32[]{:S(2)}) collective-permute-start(f32[1024,2048]{1,0:T(8,128)} %get-tuple-element.68), channel_id=1, source_target_pairs={{0,4},{4,0},{1,5},{5,1},{2,6},{6,2},{3,7},{7,3},{8,12},{12,8},{9,1... | collective-permute-start | bytes 25165832 | tf_op jit(solution)/shard_map/ppermute | solution.py:437
  564.1 182.7 %collective-permute-start.22 = (f32[1024,1024]{1,0:T(8,128)}, f32[1024,1024]{1,0:T(8,128)}, u32[]{:S(2)}, u32[]{:S(2)}) collective-permute-start(f32[1024,1024]{1,0:T(8,128)} %collective-permute-done.18.rest_2_), channel_id=1, source_target_pairs={{0,1},{1,0},{2,3},{3,2},{4,5},{5,4},{6,7},{7,6},{8,9},{9,8},{10,11... | collective-permute-start | bytes 12582920 | tf_op jit(solution)/shard_map/ppermute | solution.py:437
  565.6 181.2 %collective-permute-start.23 = (f32[1024,1024]{1,0:T(8,128)}, f32[1024,1024]{1,0:T(8,128)}, u32[]{:S(2)}, u32[]{:S(2)}) collective-permute-start(f32[1024,1024]{1,0:T(8,128)} %collective-permute-done.19.rest_3_), channel_id=1, source_target_pairs={{0,1},{1,0},{2,3},{3,2},{4,5},{5,4},{6,7},{7,6},{8,9},{9,8},{10,11... | collective-permute-start | bytes 12582920 | tf_op jit(solution)/shard_map/ppermute | solution.py:437
  744.4 195.8 %collective-permute-start.32 = (f32[2048,2048]{1,0:T(8,128)}, f32[2048,2048]{1,0:T(8,128)}, u32[]{:S(2)}, u32[]{:S(2)}) collective-permute-start(f32[2048,2048]{1,0:T(8,128)} %get-tuple-element.75), channel_id=1, source_target_pairs={{0,1},{1,0},{2,3},{3,2},{4,5},{5,4},{6,7},{7,6},{8,9},{9,8},{10,11... | collective-permute-start | bytes 50331656 | tf_op jit(solution)/shard_map/ppermute | solution.py:437
  825.6 138.4 %collective-permute-start.29 = (f32[2048,1536]{1,0:T(8,128)}, f32[2048,1536]{1,0:T(8,128)}, u32[]{:S(2)}, u32[]{:S(2)}) collective-permute-start(f32[2048,1536]{1,0:T(8,128)} %get-tuple-element.74), channel_id=1, source_target_pairs={{0,1},{1,0},{2,3},{3,2},{4,5},{5,4},{6,7},{7,6},{8,9},{9,8},{10,11... | collective-permute-start | bytes 37748744 | tf_op jit(solution)/shard_map/ppermute | solution.py:437
  825.7 114.4 %collective-permute-start.30 = (f32[1024,2048]{1,0:T(8,128)}, f32[1024,2048]{1,0:T(8,128)}, u32[]{:S(2)}, u32[]{:S(2)}) collective-permute-start(f32[1024,2048]{1,0:T(8,128)} %collective-permute-done.25.rest_3_), channel_id=1, source_target_pairs={{0,1},{1,0},{2,3},{3,2},{4,5},{5,4},{6,7},{7,6},{8,9},{9,8},{10,11... | collective-permute-start | bytes 25165832 | tf_op jit(solution)/shard_map/ppermute | solution.py:437
  826.2 114.0 %collective-permute-start.31 = (f32[1024,2048]{1,0:T(8,128)}, f32[1024,2048]{1,0:T(8,128)}, u32[]{:S(2)}, u32[]{:S(2)}) collective-permute-start(f32[1024,2048]{1,0:T(8,128)} %collective-permute-done.26.rest_4_), channel_id=1, source_target_pairs={{0,1},{1,0},{2,3},{3,2},{4,5},{5,4},{6,7},{7,6},{8,9},{9,8},{10,11... | collective-permute-start | bytes 25165832 | tf_op jit(solution)/shard_map/ppermute | solution.py:437
  829.8 90.8 %collective-permute-start.7 = (f32[512,2048]{1,0:T(8,128)}, f32[512,2048]{1,0:T(8,128)}, u32[]{:S(2)}, u32[]{:S(2)}) collective-permute-start(f32[512,2048]{1,0:T(8,128)} %get-tuple-element.51), channel_id=1, source_target_pairs={{0,8},{8,0},{1,9},{9,1},{2,10},{10,2},{3,11},{11,3},{4,12},{12,4},... | collective-permute-start | bytes 12582920 | tf_op jit(solution)/shard_map/ppermute | solution.py:437
  926.6 3.3 collective-permute-start.8
  933.2 5.1 collective-permute-start.10
  (17 other events, 672.5 us)
Sparse Core Ops, SparseCore 0:
  14.4 160.1 all-gather.1

commit v3 on v2

--- a/solution.py
+++ b/solution.py
@@ -69,17 +69,15 @@
     first = i * block
     n_sub = 4
     width = dx_ref.shape[1] // n_sub
-    per_sub = block // 128 // n_sub
+    for j in range(n_sub):
+        dx_ref[:, j * width:(j + 1) * width] += lax.dot_general(dz_buf[before], w_ref[j * width:(j + 1) * width, :], (((1,), (1,)), ((), ())), preferred_element_type=jnp.float32)
     hit_sum = t_ref[...]
-    for j in range(n_sub):
-        dz = dz_buf[before]
-        dx_ref[:, j * width:(j + 1) * width] += lax.dot_general(dz, w_ref[j * width:(j + 1) * width, :], (((1,), (1,)), ((), ())), preferred_element_type=jnp.float32)
-        for k in range(j * per_sub, (j + 1) * per_sub):
-            z = z_ref[:, k * 128:(k + 1) * 128]
-            hit = lab == lane + (first + k * 128)
-            hit_sum = hit_sum + jnp.where(hit, z, 0.0)
-            prob = jnp.exp(z - lse)
-            dz_buf[now, :, k * 128:(k + 1) * 128] = (jnp.where(hit, prob - 1.0, prob) * scale).astype(jnp.bfloat16)
+    for k in range(block // 128):
+        z = z_ref[:, k * 128:(k + 1) * 128]
+        hit = lab == lane + (first + k * 128)
+        hit_sum = hit_sum + jnp.where(hit, z, 0.0)
+        prob = jnp.exp(z - lse)
+        dz_buf[now, :, k * 128:(k + 1) * 128] = (jnp.where(hit, prob - 1.0, prob) * scale).astype(jnp.bfloat16)
     t_ref[...] = hit_sum
 
 
@@ -264,10 +262,11 @@
                         copy.start()
 
                 xt_copy(t).start()
+            if do_dw:
+                make_dw(t)
             if do_dz:
                 make_dz(t)
             if do_dw:
-                make_dw(t)
                 flush(t)
             return carry
 

time: 990 us -> 967 us (0.977)
  Pallas kernels: 627 us -> 598 us
    pallas_call x5, Pallas kernels: 426 us -> 399 us  [dw_pass(): pl.pallas_call(functools.partial(dw_kernel, n, entry, halves, len(recvs),...]
  transfers between devices with their start and end apart: 34 -> 34, of which waited for: 8 -> 8; matrix products, arithmetic and copies ran while one was open for 3% -> 3% of each run, Pallas kernels for 44% -> 43%
where the time goes in v3:
time: 967 us; the launch traced here: 960 us
  Pallas kernels  598 us (62%)
  waiting for transfers between devices  278 us (29%)
  starting transfers between devices  29.8 us (3%)
  other arithmetic  28.1 us (3%)
  between operations  17.2 us (2%)
    pallas_call x5, Pallas kernels, dw_pass(): pl.pallas_call(functools.partial(dw_kernel, n, entry, halves, len(recvs),...  399 us
    ppermute x33, waiting for transfers between devices, swap(): return lax.ppermute(v, axis, pairs)  278 us
    pallas_call x1, Pallas kernels, dx_pass(): pl.pallas_call(functools.partial(dx_kernel, n_blocks), grid=(n_blocks + 1...  74.6 us
    pallas_call x1, Pallas kernels, logits_pass(): pl.pallas_call(logits_kernel, grid=(vocab // block,), in_specs=[pl.BlockS...  66 us
    pallas_call x2, Pallas kernels, place_pass(): pl.pallas_call(functools.partial(place_kernel, tuple(tiles), len(recvs)),...  33.6 us
    ppermute x33, starting transfers between devices, swap(): return lax.ppermute(v, axis, pairs)  29.7 us
    pallas_call x1, Pallas kernels, prep_pass(): pl.pallas_call(prep_kernel, grid_spec=pltpu.PrefetchScalarGridSpec(num_sc...  25 us
  transfers between devices with their start and end apart: 34, of which 8 were waited for; matrix products, arithmetic and copies ran while one was open for 3% of the time, Pallas kernels for 43%

profile of v3, /device:TPU:1, one launch (start us, length us, event | category | flops | bytes accessed | tf_op | source)
XLA Modules:
  0.0 959.7 jit_solution(10163617849221877419)
XLA Ops:
  7.2 2.1 multiply_reduce_fusion.2
  9.4 4.9 bitcast_multiply_fusion
  16.7 2.7 collective-permute-start.4
  19.4 66.0 %logits_pass.1 = (f32[512,24576]{1,0:T(8,128)}, f32[512,128]{1,0:T(8,128)}, f32[512,128]{1,0:T(8,128)}) custom-call(bf16[512,2048]{1,0:T(8,128)(2,1)} %get-tuple-element.84.x_ref, bf16[2048,24576]{1,0:T(8,128)(2,1)} %w_ref.13), custom_call_target="tpu_custom_call" | custom-call | flops 51539607552 | bytes 150994944 | tf_op jit(solution)/shard_map/logits_pass/pallas_call | solution.py:43
  87.9 1.7 collective-permute-start
  90.5 3.1 collective-permute-start.2
  95.2 1.8 collective-permute-start.1
  97.2 3.2 collective-permute-done.1
  103.4 1.7 collective-permute-start.11
  106.2 1.3 add_add_fusion.1.bases_ref
  108.0 1.8 collective-permute-start.15
  110.5 2.0 collective-permute-start.17
  115.0 74.6 %dx_pass.1 = (f32[512,2048]{1,0:T(8,128)}, f32[512,128]{1,0:T(8,128)}) custom-call(f32[512,24576]{1,0:T(8,128)} %get-tuple-element.43.z_ref, bf16[2048,24576]{1,0:T(8,128)(2,1)} %w_ref.13, f32[512,128]{1,0:T(8,128)} %broadcast_in_dim.70.lse_ref, f32[512,128]{1,0:T(8,128)} %broadcast_in_dim.71.scale_ref, s32[512,128]{1,0:T(8,128)} %broadcast_in_dim.72.lab_ref), custom_call_target="tpu_custom_call" | custom-call | flops 51539607552 | bytes 150994944 | tf_op jit(solution)/shard_map/dx_pass/pallas_call | solution.py:89
  189.6 25.0 %prep_pass.1 = (bf16[4096,2048]{1,0:T(8,128)(2,1)}, bf16[2048,4096]{1,0:T(8,128)(2,1)}, f32[4096,128]{1,0:T(8,128)}, f32[4096,128]{1,0:T(8,128)}, s32[4096,128]{1,0:T(8,128)}) custom-call(s32[1]{0:T(128)} %bitcast.8.mine_ref, f32[4096,2048]{1,0:T(8,128)} %all-gather.2.cloned.1.call-done.x_ref, f32[1,2048]{1,0:T(1,128)} %bitcast.21, ...), custom_call_target="tpu_custom_call" | custom-call | flops 67108864 | bytes 67108864 | tf_op jit(solution)/shard_map/prep_pass/pallas_call | solution.py:126
  214.6 46.0 %shard_map.119 = (f32[2048,24576]{1,0:T(8,128)}, f32[1024,1024]{1,0:T(8,128)}, f32[1024,1024]{1,0:T(8,128)}) custom-call(s32[14]{0:T(128)} %add_add_fusion.1.bases_ref, bf16[2048,24576]{1,0:T(8,128)(2,1)} %w_ref.13, bf16[4096,2048]{1,0:T(8,128)(2,1)} %get-tuple-element.54.xn_hbm, bf16[2048,4096]{1,0:T(8,128)(2,1)} %get-tuple-element.55.xt_hbm, ...), custom_call_target="tpu_custom_call" | custom-call | flops 34359738368 | bytes 20971520 | tf_op jit(solution)/shard_map/pallas_call | solution.py:347
  261.6 84.6 %shard_map.120 = (f32[2048,24576]{1,0:T(8,128)}, f32[1024,2048]{1,0:T(8,128)}, f32[1024,2048]{1,0:T(8,128)}) custom-call(s32[14]{0:T(128)} %add_add_fusion.1.bases_ref, bf16[2048,24576]{1,0:T(8,128)(2,1)} %w_ref.13, bf16[4096,2048]{1,0:T(8,128)(2,1)} %get-tuple-element.54.xn_hbm, ...), custom_call_target="tpu_custom_call", output_to_operand_aliasing={{0}: (7, {})} | custom-call | flops 68719476736 | bytes 41943040 | tf_op jit(solution)/shard_map/pallas_call | solution.py:347
  346.3 105.4 %shard_map.121 = (f32[2048,24576]{1,0:T(8,128)}, f32[2048,2560]{1,0:T(8,128)}) custom-call(s32[14]{0:T(128)} %add_add_fusion.1.bases_ref, bf16[2048,24576]{1,0:T(8,128)(2,1)} %w_ref.13, bf16[4096,2048]{1,0:T(8,128)(2,1)} %get-tuple-element.54.xn_hbm, bf16[2048,4096]{1,0:T(8,128)(2,1)} %get-tuple-element.55.xt_hbm, ...), custom_call_target="tpu_custom_call", output_to_operand_aliasing={{0}: (9, {})} | custom-call | flops 85899345920 | bytes 52428800 | tf_op jit(solution)/shard_map/pallas_call | solution.py:347
  454.0 91.1 %collective-permute-done.18.rest_2_ = f32[1024,1024]{1,0:T(8,128)} collective-permute-done((f32[1024,1024]{1,0:T(8,128)}, f32[1024,1024]{1,0:T(8,128)}, u32[]{:S(2)}, u32[]{:S(2)}) %collective-permute-start.18) | collective-permute-done | bytes 4194336 | tf_op jit(solution)/shard_map/ppermute | solution.py:436
  546.4 1.5 collective-permute-start.22
  547.9 88.8 %shard_map.122 = (f32[2048,24576]{1,0:T(8,128)}, f32[2048,2048]{1,0:T(8,128)}) custom-call(s32[14]{0:T(128)} %add_add_fusion.1.bases_ref, bf16[2048,24576]{1,0:T(8,128)(2,1)} %w_ref.13, bf16[4096,2048]{1,0:T(8,128)(2,1)} %get-tuple-element.54.xn_hbm, bf16[2048,4096]{1,0:T(8,128)(2,1)} %get-tuple-element.55.xt_hbm, ...), custom_call_target="tpu_custom_call", output_to_operand_aliasing={{0}: (11, {})} | custom-call | flops 68719476736 | bytes 41943040 | tf_op jit(solution)/shard_map/pallas_call | solution.py:347
  636.7 89.8 %collective-permute-done.25.rest_3_ = f32[1024,2048]{1,0:T(8,128)} collective-permute-done((f32[1024,2048]{1,0:T(8,128)}, f32[1024,2048]{1,0:T(8,128)}, u32[]{:S(2)}, u32[]{:S(2)}) %collective-permute-start.25) | collective-permute-done | bytes 8388640 | tf_op jit(solution)/shard_map/ppermute | solution.py:436
  727.5 2.0 collective-permute-start.32
  729.5 74.2 %shard_map.123 = (f32[2048,24576]{1,0:T(8,128)}, f32[2048,1536]{1,0:T(8,128)}) custom-call(s32[14]{0:T(128)} %add_add_fusion.1.bases_ref, bf16[2048,24576]{1,0:T(8,128)(2,1)} %w_ref.13, bf16[4096,2048]{1,0:T(8,128)(2,1)} %get-tuple-element.54.xn_hbm, bf16[2048,4096]{1,0:T(8,128)(2,1)} %get-tuple-element.55.xt_hbm, ...), custom_call_target="tpu_custom_call", output_to_operand_aliasing={{0}: (12, {})} | custom-call | flops 51539607552 | bytes 31457280 | tf_op jit(solution)/shard_map/pallas_call | solution.py:347
  805.9 2.0 collective-permute-done.6
  808.4 1.3 select_reduce_fusion.1
  809.8 89.0 %collective-permute-done.7 = f32[512,2048]{1,0:T(8,128)} collective-permute-done((f32[512,2048]{1,0:T(8,128)}, f32[512,2048]{1,0:T(8,128)}, u32[]{:S(2)}, u32[]{:S(2)}) %collective-permute-start.7) | collective-permute-done | bytes 4194336 | tf_op jit(solution)/shard_map/ppermute | solution.py:436
  898.7 5.3 multiply_reduce_fusion
  904.7 2.5 collective-permute-start.8
  909.1 2.3 collective-permute-done.9
  911.4 4.6 multiply_convert_fusion
  917.9 23.9 %place_pass.2.rest_1_ = f32[2048,24576]{1,0:T(8,128)} custom-call(s32[14]{0:T(128)} %add_add_fusion.1.bases_ref, f32[1024,2048]{1,0:T(8,128)} %collective-permute-done.30.rest_0_, f32[1024,2048]{1,0:T(8,128)} %collective-permute-done.31.rest_1_, f32[2048,2048]{1,0:T(8,128)} %collective-permute-done.32.rest_2_, ...), custom_call_target="tpu_custom_call", output_to_operand_aliasing={{}: (4, {})} | custom-call | flops 335544320 | bytes 67108864 | tf_op jit(solution)/shard_map/place_pass/pallas_call | solution.py:399
  941.8 9.7 %place_pass.3 = f32[2048,24576]{1,0:T(8,128)} custom-call(s32[14]{0:T(128)} %add_add_fusion.1.bases_ref, f32[2048,1536]{1,0:T(8,128)} %collective-permute-done.29.rest_0_, f32[2048,24576]{1,0:T(8,128)} %place_pass.2.rest_1_), custom_call_target="tpu_custom_call", output_to_operand_aliasing={{}: (2, {})} | custom-call | flops 125829120 | bytes 25165824 | tf_op jit(solution)/shard_map/place_pass/pallas_call | solution.py:399
  (122 shorter events, 26.8 us)
Async XLA Ops:
  7.2 182.4 %all-gather.2.cloned.1.call-start = ((), (), s32[]{:S(2)}) async-start(), calls=%async_computation | async-start | bytes 37748736 | tf_op jit(solution)/shard_map/all_gather | solution.py:442
  16.7 84.0 %collective-permute-start.3 = (f32[128]{0:T(128)}, f32[128]{0:T(128)}, u32[]{:S(2)}, u32[]{:S(2)}) collective-permute-start(f32[128]{0:T(128)} %broadcast_in_dim.69), channel_id=1, source_target_pairs={{0,1},{1,0},{2,3},{3,2},{4,5},{5,4},{6,7},{7,6},{8,9},{9,8},{10,11... | collective-permute-start | bytes 1544 | tf_op jit(solution)/shard_map/ppermute | solution.py:436
  16.7 84.0 %collective-permute-start.4 = (f32[128]{0:T(128)}, f32[128]{0:T(128)}, u32[]{:S(2)}, u32[]{:S(2)}) collective-permute-start(f32[128]{0:T(128)} %broadcast_in_dim.69), channel_id=1, source_target_pairs={{0,2},{1,3},{2,0},{3,1},{4,6},{5,7},{6,4},{7,5},{8,10},{9,11},{10,... | collective-permute-start | bytes 1544 | tf_op jit(solution)/shard_map/ppermute | solution.py:436
  19.4 81.3 %collective-permute-start.5 = (f32[128]{0:T(128)}, f32[128]{0:T(128)}, u32[]{:S(2)}, u32[]{:S(2)}) collective-permute-start(f32[128]{0:T(128)} %broadcast_in_dim.69), channel_id=1, source_target_pairs={{0,3},{1,2},{2,1},{3,0},{4,7},{5,6},{6,5},{7,4},{8,11},{9,10},{10,... | collective-permute-start | bytes 1544 | tf_op jit(solution)/shard_map/ppermute | solution.py:436
  87.9 14.8 %collective-permute-start = (f32[2,512]{1,0:T(2,128)S(1)}, f32[2,512]{1,0:T(2,128)S(1)}, u32[]{:S(2)}, u32[]{:S(2)}) collective-permute-start(f32[2,512]{1,0:T(2,128)S(1)} %pad_maximum_fusion.1), channel_id=1, source_target_pairs={{0,8},{8,0},{1,9},{9,1},{2,10},{10,2},{3,11},{11,3},{4,12},{12,4},... | collective-permute-start | bytes 12296 | tf_op jit(solution)/shard_map/ppermute | solution.py:436
  90.5 4.8 collective-permute-start.2
  95.2 5.1 collective-permute-start.1
  103.4 6.5 collective-permute-start.11
  105.1 5.4 collective-permute-start.12
  107.5 82.1 %collective-permute-start.13 = (f32[3,512]{1,0:T(4,128)}, f32[3,512]{1,0:T(4,128)}, u32[]{:S(2)}, u32[]{:S(2)}) collective-permute-start(f32[3,512]{1,0:T(4,128)} %pad_maximum_fusion.refs_0_), channel_id=1, source_target_pairs={{0,3},{1,2},{2,1},{3,0},{4,7},{5,6},{6,5},{7,4},{8,11},{9,10},{10,... | collective-permute-start | bytes 18440 | tf_op jit(solution)/shard_map/ppermute | solution.py:436
  108.0 81.6 %collective-permute-start.14 = (f32[3,512]{1,0:T(4,128)}, f32[3,512]{1,0:T(4,128)}, u32[]{:S(2)}, u32[]{:S(2)}) collective-permute-start(f32[3,512]{1,0:T(4,128)} %pad_maximum_fusion.refs_0_), channel_id=1, source_target_pairs={{0,4},{1,5},{2,6},{3,7},{4,0},{5,1},{6,2},{7,3},{8,12},{9,13},{10,... | collective-permute-start | bytes 18440 | tf_op jit(solution)/shard_map/ppermute | solution.py:436
  108.0 81.6 %collective-permute-start.15 = (f32[3,512]{1,0:T(4,128)}, f32[3,512]{1,0:T(4,128)}, u32[]{:S(2)}, u32[]{:S(2)}) collective-permute-start(f32[3,512]{1,0:T(4,128)} %pad_maximum_fusion.refs_0_), channel_id=1, source_target_pairs={{0,5},{1,4},{2,7},{3,6},{4,1},{5,0},{6,3},{7,2},{8,13},{9,12},{10,... | collective-permute-start | bytes 18440 | tf_op jit(solution)/shard_map/ppermute | solution.py:436
  109.8 79.8 %collective-permute-start.16 = (f32[3,512]{1,0:T(4,128)}, f32[3,512]{1,0:T(4,128)}, u32[]{:S(2)}, u32[]{:S(2)}) collective-permute-start(f32[3,512]{1,0:T(4,128)} %pad_maximum_fusion.refs_0_), channel_id=1, source_target_pairs={{0,6},{1,7},{2,4},{3,5},{4,2},{5,3},{6,0},{7,1},{8,14},{9,15},{10,... | collective-permute-start | bytes 18440 | tf_op jit(solution)/shard_map/ppermute | solution.py:436
  110.5 79.2 %collective-permute-start.17 = (f32[3,512]{1,0:T(4,128)}, f32[3,512]{1,0:T(4,128)}, u32[]{:S(2)}, u32[]{:S(2)}) collective-permute-start(f32[3,512]{1,0:T(4,128)} %pad_maximum_fusion.refs_0_), channel_id=1, source_target_pairs={{0,7},{1,6},{2,5},{3,4},{4,3},{5,2},{6,1},{7,0},{8,15},{9,14},{10,... | collective-permute-start | bytes 18440 | tf_op jit(solution)/shard_map/ppermute | solution.py:436
  260.6 85.7 %collective-permute-start.20 = (f32[1024,1024]{1,0:T(8,128)}, f32[1024,1024]{1,0:T(8,128)}, u32[]{:S(2)}, u32[]{:S(2)}) collective-permute-start(f32[1024,1024]{1,0:T(8,128)} %get-tuple-element.59), channel_id=1, source_target_pairs={{0,1},{1,0},{2,3},{3,2},{4,5},{5,4},{6,7},{7,6},{8,9},{9,8},{10,11... | collective-permute-start | bytes 12582920 | tf_op jit(solution)/shard_map/ppermute | solution.py:436
  261.6 84.7 %collective-permute-start.21 = (f32[1024,1024]{1,0:T(8,128)}, f32[1024,1024]{1,0:T(8,128)}, u32[]{:S(2)}, u32[]{:S(2)}) collective-permute-start(f32[1024,1024]{1,0:T(8,128)} %get-tuple-element.60), channel_id=1, source_target_pairs={{0,1},{1,0},{2,3},{3,2},{4,5},{5,4},{6,7},{7,6},{8,9},{9,8},{10,11... | collective-permute-start | bytes 12582920 | tf_op jit(solution)/shard_map/ppermute | solution.py:436
  451.7 277.8 %collective-permute-start.24 = (f32[2048,2560]{1,0:T(8,128)}, f32[2048,2560]{1,0:T(8,128)}, u32[]{:S(2)}, u32[]{:S(2)}) collective-permute-start(f32[2048,2560]{1,0:T(8,128)} %get-tuple-element.66), channel_id=1, source_target_pairs={{0,1},{1,0},{2,3},{3,2},{4,5},{5,4},{6,7},{7,6},{8,9},{9,8},{10,11... | collective-permute-start | bytes 62914568 | tf_op jit(solution)/shard_map/ppermute | solution.py:436
  452.2 94.2 %collective-permute-start.27 = (f32[1024,2048]{1,0:T(8,128)}, f32[1024,2048]{1,0:T(8,128)}, u32[]{:S(2)}, u32[]{:S(2)}) collective-permute-start(f32[1024,2048]{1,0:T(8,128)} %get-tuple-element.67), channel_id=1, source_target_pairs={{0,1},{1,0},{2,3},{3,2},{4,5},{5,4},{6,7},{7,6},{8,9},{9,8},{10,11... | collective-permute-start | bytes 25165832 | tf_op jit(solution)/shard_map/ppermute | solution.py:436
  452.3 95.6 %collective-permute-start.28 = (f32[1024,2048]{1,0:T(8,128)}, f32[1024,2048]{1,0:T(8,128)}, u32[]{:S(2)}, u32[]{:S(2)}) collective-permute-start(f32[1024,2048]{1,0:T(8,128)} %get-tuple-element.68), channel_id=1, source_target_pairs={{0,1},{1,0},{2,3},{3,2},{4,5},{5,4},{6,7},{7,6},{8,9},{9,8},{10,11... | collective-permute-start | bytes 25165832 | tf_op jit(solution)/shard_map/ppermute | solution.py:436
  452.7 92.4 %collective-permute-start.18 = (f32[1024,1024]{1,0:T(8,128)}, f32[1024,1024]{1,0:T(8,128)}, u32[]{:S(2)}, u32[]{:S(2)}) collective-permute-start(f32[1024,1024]{1,0:T(8,128)} %get-tuple-element.59), channel_id=1, source_target_pairs={{0,2},{1,3},{2,0},{3,1},{4,6},{5,7},{6,4},{7,5},{8,10},{9,11},{10,... | collective-permute-start | bytes 12582920 | tf_op jit(solution)/shard_map/ppermute | solution.py:436
  453.9 92.4 %collective-permute-start.19 = (f32[1024,1024]{1,0:T(8,128)}, f32[1024,1024]{1,0:T(8,128)}, u32[]{:S(2)}, u32[]{:S(2)}) collective-permute-start(f32[1024,1024]{1,0:T(8,128)} %get-tuple-element.60), channel_id=1, source_target_pairs={{0,4},{4,0},{1,5},{5,1},{2,6},{6,2},{3,7},{7,3},{8,12},{12,8},{9,1... | collective-permute-start | bytes 12582920 | tf_op jit(solution)/shard_map/ppermute | solution.py:436
  545.1 181.4 %collective-permute-start.25 = (f32[1024,2048]{1,0:T(8,128)}, f32[1024,2048]{1,0:T(8,128)}, u32[]{:S(2)}, u32[]{:S(2)}) collective-permute-start(f32[1024,2048]{1,0:T(8,128)} %get-tuple-element.67), channel_id=1, source_target_pairs={{0,2},{1,3},{2,0},{3,1},{4,6},{5,7},{6,4},{7,5},{8,10},{9,11},{10,... | collective-permute-start | bytes 25165832 | tf_op jit(solution)/shard_map/ppermute | solution.py:436
  546.3 181.1 %collective-permute-start.26 = (f32[1024,2048]{1,0:T(8,128)}, f32[1024,2048]{1,0:T(8,128)}, u32[]{:S(2)}, u32[]{:S(2)}) collective-permute-start(f32[1024,2048]{1,0:T(8,128)} %get-tuple-element.68), channel_id=1, source_target_pairs={{0,4},{4,0},{1,5},{5,1},{2,6},{6,2},{3,7},{7,3},{8,12},{12,8},{9,1... | collective-permute-start | bytes 25165832 | tf_op jit(solution)/shard_map/ppermute | solution.py:436
  546.4 183.1 %collective-permute-start.22 = (f32[1024,1024]{1,0:T(8,128)}, f32[1024,1024]{1,0:T(8,128)}, u32[]{:S(2)}, u32[]{:S(2)}) collective-permute-start(f32[1024,1024]{1,0:T(8,128)} %collective-permute-done.18.rest_2_), channel_id=1, source_target_pairs={{0,1},{1,0},{2,3},{3,2},{4,5},{5,4},{6,7},{7,6},{8,9},{9,8},{10,11... | collective-permute-start | bytes 12582920 | tf_op jit(solution)/shard_map/ppermute | solution.py:436
  547.9 181.6 %collective-permute-start.23 = (f32[1024,1024]{1,0:T(8,128)}, f32[1024,1024]{1,0:T(8,128)}, u32[]{:S(2)}, u32[]{:S(2)}) collective-permute-start(f32[1024,1024]{1,0:T(8,128)} %collective-permute-done.19.rest_3_), channel_id=1, source_target_pairs={{0,1},{1,0},{2,3},{3,2},{4,5},{5,4},{6,7},{7,6},{8,9},{9,8},{10,11... | collective-permute-start | bytes 12582920 | tf_op jit(solution)/shard_map/ppermute | solution.py:436
  727.5 190.4 %collective-permute-start.32 = (f32[2048,2048]{1,0:T(8,128)}, f32[2048,2048]{1,0:T(8,128)}, u32[]{:S(2)}, u32[]{:S(2)}) collective-permute-start(f32[2048,2048]{1,0:T(8,128)} %get-tuple-element.75), channel_id=1, source_target_pairs={{0,1},{1,0},{2,3},{3,2},{4,5},{5,4},{6,7},{7,6},{8,9},{9,8},{10,11... | collective-permute-start | bytes 50331656 | tf_op jit(solution)/shard_map/ppermute | solution.py:436
  803.7 138.0 %collective-permute-start.29 = (f32[2048,1536]{1,0:T(8,128)}, f32[2048,1536]{1,0:T(8,128)}, u32[]{:S(2)}, u32[]{:S(2)}) collective-permute-start(f32[2048,1536]{1,0:T(8,128)} %get-tuple-element.74), channel_id=1, source_target_pairs={{0,1},{1,0},{2,3},{3,2},{4,5},{5,4},{6,7},{7,6},{8,9},{9,8},{10,11... | collective-permute-start | bytes 37748744 | tf_op jit(solution)/shard_map/ppermute | solution.py:436
  803.8 114.1 %collective-permute-start.30 = (f32[1024,2048]{1,0:T(8,128)}, f32[1024,2048]{1,0:T(8,128)}, u32[]{:S(2)}, u32[]{:S(2)}) collective-permute-start(f32[1024,2048]{1,0:T(8,128)} %collective-permute-done.25.rest_3_), channel_id=1, source_target_pairs={{0,1},{1,0},{2,3},{3,2},{4,5},{5,4},{6,7},{7,6},{8,9},{9,8},{10,11... | collective-permute-start | bytes 25165832 | tf_op jit(solution)/shard_map/ppermute | solution.py:436
  804.3 113.6 %collective-permute-start.31 = (f32[1024,2048]{1,0:T(8,128)}, f32[1024,2048]{1,0:T(8,128)}, u32[]{:S(2)}, u32[]{:S(2)}) collective-permute-start(f32[1024,2048]{1,0:T(8,128)} %collective-permute-done.26.rest_4_), channel_id=1, source_target_pairs={{0,1},{1,0},{2,3},{3,2},{4,5},{5,4},{6,7},{7,6},{8,9},{9,8},{10,11... | collective-permute-start | bytes 25165832 | tf_op jit(solution)/shard_map/ppermute | solution.py:436
  807.9 90.8 %collective-permute-start.7 = (f32[512,2048]{1,0:T(8,128)}, f32[512,2048]{1,0:T(8,128)}, u32[]{:S(2)}, u32[]{:S(2)}) collective-permute-start(f32[512,2048]{1,0:T(8,128)} %get-tuple-element.51), channel_id=1, source_target_pairs={{0,8},{8,0},{1,9},{9,1},{2,10},{10,2},{3,11},{11,3},{4,12},{12,4},... | collective-permute-start | bytes 12582920 | tf_op jit(solution)/shard_map/ppermute | solution.py:436
  904.7 3.3 collective-permute-start.8
  911.3 4.7 collective-permute-start.10
  (17 other events, 675.1 us)
Sparse Core Ops, SparseCore 0:
  14.4 160.1 all-gather.1
